TPU v7x, 8 devices: a whole 2x2x1 slice. The times are simulated.
8 devices in a mesh: case: 1 (over z), model: 2 (over y), ens: 4 (over x, core).
Axes of the slice: x: 2, y: 2, z: 1, core: 2. Of those that a mesh axis runs over, the one named last changes fastest.
Arguments:
- ens_init: float32 [16, 5120, 64], P(('case', 'ens'), None, 'model')
- mix_op: bfloat16 [5120, 5120], replicated
- w_in: bfloat16 [3, 64, 1024], P(None, None, 'model')
- w_out: bfloat16 [3, 1024, 64], P(None, 'model')
- obs_val: float32 [2, 5120, 32], P(None, ('case', 'ens', 'model'))
- obs_prec: float32 [5120, 32], P(('case', 'ens', 'model'))
- obs_idx: int32 [32], replicated
- inflation: float32 [1], replicated
Outputs:
- output: float32 [16, 5120, 64], P(('case', 'ens'), None, 'model')
All inputs are finite; a program needn't handle non-finite values.
Results may differ from a plain program's by a relative error of at most 0.0151655.
Values are sent between devices in bfloat16 or wider.
A program may use at most 1 GiB of HBM per device.

v0:
```python
import jax
import jax.numpy as jnp
from jax import lax
from jax.sharding import PartitionSpec as P

NS_STEPS = 12
FULL_PREC = lax.Precision.HIGHEST


def value_a8(ens_state, mix_op, w_in, w_out):
    for layer_idx in range(w_in.shape[0]):
        mix_out = jnp.einsum('ij,jkc->ikc', mix_op, ens_state.astype(jnp.bfloat16), preferred_element_type=jnp.float32).astype(jnp.bfloat16)
        mix_full = lax.all_gather(mix_out, 'model', axis=2, tiled=True)
        hidden = jax.nn.gelu(jnp.einsum('ikv,vf->ikf', mix_full, w_in[layer_idx], preferred_element_type=jnp.float32), approximate=True)
        part_sum = jnp.einsum('ikf,fv->ikv', hidden.astype(jnp.bfloat16), w_out[layer_idx], preferred_element_type=jnp.float32)
        ens_state = ens_state + lax.psum_scatter(part_sum, 'model', scatter_dimension=2, tiled=True)
    return ens_state


def letkf_weights(col_state, obs_now, prec_now, obs_idx, inflation):
    members = col_state.shape[-2]
    ens_mean = jnp.mean(col_state, axis=-2)
    anomaly = col_state - ens_mean[..., None, :]
    obs_anom = jnp.take(anomaly, obs_idx, axis=-1)
    innovation = obs_now - jnp.take(ens_mean, obs_idx, axis=-1)
    weighted = obs_anom * prec_now[..., None, :]
    identity = jnp.eye(members, dtype=jnp.float32)
    a_tilde = ((members - 1) / inflation[0]) * identity + jnp.einsum('...ip,...jp->...ij', weighted, obs_anom, precision=FULL_PREC)
    trace_sum = jnp.trace(a_tilde, axis1=-2, axis2=-1)[..., None, None]
    b_mat = a_tilde / trace_sum
    t_mat = 1.5 * identity - 0.5 * b_mat
    z_mat = t_mat
    for ns_step in range(1, NS_STEPS):
        b_mat = jnp.matmul(b_mat, t_mat, precision=FULL_PREC)
        t_mat = 1.5 * identity - 0.5 * jnp.matmul(z_mat, b_mat, precision=FULL_PREC)
        z_mat = jnp.matmul(t_mat, z_mat, precision=FULL_PREC)
    sqrt_inv = z_mat / jnp.sqrt(trace_sum)
    gain_vec = jnp.einsum('...ip,...p->...i', weighted, innovation, precision=FULL_PREC)
    half_step = jnp.einsum('...ij,...j->...i', sqrt_inv, gain_vec, precision=FULL_PREC)
    w_mean = jnp.einsum('...ij,...j->...i', sqrt_inv, half_step, precision=FULL_PREC)
    w_full = (members - 1) ** 0.5 * sqrt_inv + w_mean[..., None]
    return ens_mean, anomaly, w_full


def solution(mesh):
    def local_step(ens_local, mix_op, w_in, w_out, obs_val, obs_prec, obs_idx, inflation):
        ens_state = jnp.transpose(ens_local, (1, 0, 2))
        for cycle_idx in range(obs_val.shape[0]):
            ens_state = value_a8(ens_state, mix_op, w_in, w_out)
            col_state = lax.all_to_all(ens_state, 'ens', 0, 1, tiled=True)
            col_state = lax.all_to_all(col_state, 'model', 0, 2, tiled=True)
            ens_mean, anomaly, w_full = letkf_weights(col_state, obs_val[cycle_idx], obs_prec, obs_idx, inflation)
            col_state = ens_mean[:, None, :] + jnp.einsum('bik,biv->bkv', w_full, anomaly, precision=FULL_PREC)
            col_state = lax.all_to_all(col_state, 'model', 2, 0, tiled=True)
            ens_state = lax.all_to_all(col_state, 'ens', 1, 0, tiled=True)
        return jnp.transpose(ens_state, (1, 0, 2))

    member_spec = P(('case', 'ens'), None, 'model')
    col_axes = ('case', 'ens', 'model')
    in_specs = (member_spec, P(None, None), P(None, None, 'model'), P(None, 'model', None), P(None, col_axes, None), P(col_axes, None), P(None), P(None))
    return jax.shard_map(local_step, mesh=mesh, in_specs=in_specs, out_specs=member_spec, check_vma=False)
```

profile of v0, /device:TPU:0, one launch (start us, length us, event | category | flops | bytes accessed | tf_op | source)
XLA Modules:
  0.0 2018.5 jit_solution(9847164401771509673)
XLA Ops:
  32.7 39.1 %all-gather.7.cloned.1.call-done = bf16[5120,4,64]{0,2,1:T(8,128)(2,1)} async-done(((bf16[5120,4,32]{0,2,1:T(8,128)(2,1)}), bf16[5120,4,64]{0,2,1:T(8,128)(2,1)}) %all-gather.7.cloned.1.call-update) | async-done | bytes 2621456 | tf_op jit(solution)/shard_map/all_gather | solution.py:13
  89.8 62.8 %reduce-scatter.7.cloned.1.call-done = f32[5120,4,32]{0,2,1:T(8,128)} async-done(((f32[5120,4,64]{0,2,1:T(8,128)}), f32[5120,4,32]{0,2,1:T(8,128)}) %reduce-scatter.7.cloned.1.call-update) | async-done | bytes 2621456 | tf_op jit(solution)/shard_map/reduce_scatter | solution.py:16
  152.6 24.5 %fusion.97 = bf16[5120,4,32]{0,2,1:T(8,128)(2,1)} fusion(bf16[5120,5120]{1,0:T(8,128)(2,1)} %param.13, f32[5120,4,32]{0,2,1:T(8,128)} %reduce-scatter.7.cloned.1.call-done, f32[4,5120,32]{1,2,0:T(8,128)S(1)} %copy-done), kind=kOutput, calls=%fused_computation.83 | convolution fusion | flops 6712852480 | bytes 58982400 | tf_op jit(solution)/shard_map/ij,jkc->ikc/dot_general | solution.py:12
  177.2 36.3 %all-gather.9.cloned.1.call-done = bf16[5120,4,64]{0,2,1:T(8,128)(2,1)} async-done(((bf16[5120,4,32]{0,2,1:T(8,128)(2,1)}), bf16[5120,4,64]{0,2,1:T(8,128)(2,1)}) %all-gather.9.cloned.1.call-update) | async-done | bytes 2621456 | tf_op jit(solution)/shard_map/all_gather | solution.py:13
  231.4 62.8 %reduce-scatter.9.cloned.1.call-done = f32[5120,4,32]{0,2,1:T(8,128)} async-done(((f32[5120,4,64]{0,2,1:T(8,128)}), f32[5120,4,32]{0,2,1:T(8,128)}) %reduce-scatter.9.cloned.1.call-update) | async-done | bytes 2621456 | tf_op jit(solution)/shard_map/reduce_scatter | solution.py:16
  294.2 25.4 %fusion.94 = bf16[5120,4,32]{0,2,1:T(8,128)(2,1)} fusion(bf16[5120,5120]{1,0:T(8,128)(2,1)} %param.13, f32[5120,4,32]{0,2,1:T(8,128)} %reduce-scatter.9.cloned.1.call-done, f32[5120,4,32]{0,2,1:T(8,128)} %reduce-scatter.7.cloned.1.call-done, f32[4,5120,32]{1,2,0:T(8,128)S(1)} %copy-done), kind=kOutput, calls=%fused_computation.82 | convolution fusion | flops 6713507840 | bytes 61603840 | tf_op jit(solution)/shard_map/ij,jkc->ikc/dot_general | solution.py:12
  319.6 36.3 %all-gather.11.cloned.1.call-done = bf16[5120,4,64]{0,2,1:T(8,128)(2,1)} async-done(((bf16[5120,4,32]{0,2,1:T(8,128)(2,1)}), bf16[5120,4,64]{0,2,1:T(8,128)(2,1)}) %all-gather.11.cloned.1.call-update) | async-done | bytes 2621456 | tf_op jit(solution)/shard_map/all_gather | solution.py:13
  373.6 63.0 %reduce-scatter.11.cloned.1.call-done = f32[5120,4,32]{0,2,1:T(8,128)} async-done(((f32[5120,4,64]{0,2,1:T(8,128)}), f32[5120,4,32]{0,2,1:T(8,128)}) %reduce-scatter.11.cloned.1.call-update) | async-done | bytes 2621456 | tf_op jit(solution)/shard_map/reduce_scatter | solution.py:16
  460.3 35.1 %all_to_all.144 = f32[4,1,163840]{2,1,0:T(1,128)S(1)} all-to-all(f32[4,1,163840]{2,1,0:T(1,128)} %reshape.121), channel_id=1, replica_groups=mesh['case'=1,'model'=2,'ens'=4] {'ens'}, dimensions={0} | all-to-all | bytes 5242880 | tf_op jit(solution)/shard_map/all_to_all | solution.py:50
  548.3 29.3 %all-to-all-done.1 = f32[2,1,327680]{2,1,0:T(1,128)S(1)} async-done(((f32[2,1,327680]{2,1,0:T(1,128)}), f32[2,1,327680]{2,1,0:T(1,128)S(1)}, u32[]{:S(2)}, u32[]{:S(2)}) %all-to-all-start.1) | async-done | bytes 2621472 | tf_op jit(solution)/shard_map/all_to_all | solution.py:51
  936.6 32.1 %all_to_all.145 = f32[640,16,64]{0,1,2:T(8,128)S(1)} all-to-all(f32[640,16,64]{0,1,2:T(8,128)S(1)} %copy.134), channel_id=1, replica_groups=mesh['case'=1,'model'=2,'ens'=4] {'model'}, dimensions={2} | all-to-all | bytes 5242880 | tf_op jit(solution)/shard_map/all_to_all | solution.py:54
  973.9 35.1 %all_to_all.146 = f32[1280,16,32]{0,2,1:T(8,128)S(1)} all-to-all(f32[1280,16,32]{0,2,1:T(8,128)} %all_to_all.115), channel_id=1, replica_groups=mesh['case'=1,'model'=2,'ens'=4] {'ens'}, dimensions={1} | all-to-all | bytes 5242880 | tf_op jit(solution)/shard_map/all_to_all | solution.py:55
  1033.5 35.2 %all-gather.13.cloned.1.call-done = bf16[5120,4,64]{0,2,1:T(8,128)(2,1)} async-done(((bf16[5120,4,32]{0,2,1:T(8,128)(2,1)}), bf16[5120,4,64]{0,2,1:T(8,128)(2,1)}) %all-gather.13.cloned.1.call-update) | async-done | bytes 2621456 | tf_op jit(solution)/shard_map/all_gather | solution.py:13
  1086.4 63.0 %reduce-scatter.13.cloned.1.call-done = f32[5120,4,32]{0,2,1:T(8,128)} async-done(((f32[5120,4,64]{0,2,1:T(8,128)}), f32[5120,4,32]{0,2,1:T(8,128)}) %reduce-scatter.13.cloned.1.call-update) | async-done | bytes 2621456 | tf_op jit(solution)/shard_map/reduce_scatter | solution.py:16
  1152.9 24.7 %fusion.88 = bf16[5120,4,32]{0,2,1:T(8,128)(2,1)} fusion(bf16[5120,5120]{1,0:T(8,128)(2,1)} %param.13, f32[5120,4,32]{0,2,1:T(8,128)} %add.141), kind=kOutput, calls=%fused_computation.80 | convolution fusion | flops 6712197120 | bytes 56360960 | tf_op jit(solution)/shard_map/ij,jkc->ikc/dot_general | solution.py:12
  1177.7 36.2 %all-gather.15.cloned.1.call-done = bf16[5120,4,64]{0,2,1:T(8,128)(2,1)} async-done(((bf16[5120,4,32]{0,2,1:T(8,128)(2,1)}), bf16[5120,4,64]{0,2,1:T(8,128)(2,1)}) %all-gather.15.cloned.1.call-update) | async-done | bytes 2621456 | tf_op jit(solution)/shard_map/all_gather | solution.py:13
  1231.7 63.0 %reduce-scatter.15.cloned.1.call-done = f32[5120,4,32]{0,2,1:T(8,128)} async-done(((f32[5120,4,64]{0,2,1:T(8,128)}), f32[5120,4,32]{0,2,1:T(8,128)}) %reduce-scatter.15.cloned.1.call-update) | async-done | bytes 2621456 | tf_op jit(solution)/shard_map/reduce_scatter | solution.py:16
  1298.2 24.7 %fusion.85 = bf16[5120,4,32]{0,2,1:T(8,128)(2,1)} fusion(bf16[5120,5120]{1,0:T(8,128)(2,1)} %param.13, f32[5120,4,32]{0,2,1:T(8,128)} %add.144), kind=kOutput, calls=%fused_computation.79 | convolution fusion | flops 6712197120 | bytes 56360960 | tf_op jit(solution)/shard_map/ij,jkc->ikc/dot_general | solution.py:12
  1323.0 36.3 %all-gather.17.cloned.1.call-done = bf16[5120,4,64]{0,2,1:T(8,128)(2,1)} async-done(((bf16[5120,4,32]{0,2,1:T(8,128)(2,1)}), bf16[5120,4,64]{0,2,1:T(8,128)(2,1)}) %all-gather.17.cloned.1.call-update) | async-done | bytes 2621456 | tf_op jit(solution)/shard_map/all_gather | solution.py:13
  1376.9 63.0 %reduce-scatter.17.cloned.1.call-done = f32[5120,4,32]{0,2,1:T(8,128)} async-done(((f32[5120,4,64]{0,2,1:T(8,128)}), f32[5120,4,32]{0,2,1:T(8,128)}) %reduce-scatter.17.cloned.1.call-update) | async-done | bytes 2621456 | tf_op jit(solution)/shard_map/reduce_scatter | solution.py:16
  1461.7 35.1 %all_to_all.147 = f32[4,1,163840]{2,1,0:T(1,128)S(1)} all-to-all(f32[4,1,163840]{2,1,0:T(1,128)} %reshape.125), channel_id=1, replica_groups=mesh['case'=1,'model'=2,'ens'=4] {'ens'}, dimensions={0} | all-to-all | bytes 5242880 | tf_op jit(solution)/shard_map/all_to_all | solution.py:50
  1544.3 34.1 %all_to_all.148 = f32[2,1,327680]{2,1,0:T(1,128)S(1)} all-to-all(f32[2,1,327680]{2,1,0:T(1,128)} %reshape.127), channel_id=1, replica_groups=mesh['case'=1,'model'=2,'ens'=4] {'model'}, dimensions={0} | all-to-all | bytes 5242880 | tf_op jit(solution)/shard_map/all_to_all | solution.py:51
  1937.6 32.1 %all_to_all.149 = f32[640,16,64]{0,1,2:T(8,128)S(1)} all-to-all(f32[640,16,64]{0,1,2:T(8,128)S(1)} %copy.151), channel_id=1, replica_groups=mesh['case'=1,'model'=2,'ens'=4] {'model'}, dimensions={2} | all-to-all | bytes 5242880 | tf_op jit(solution)/shard_map/all_to_all | solution.py:54
  1975.0 34.7 %all_to_all.150 = f32[1280,16,32]{0,2,1:T(8,128)S(1)} all-to-all(f32[1280,16,32]{0,2,1:T(8,128)} %all_to_all.131), channel_id=1, replica_groups=mesh['case'=1,'model'=2,'ens'=4] {'ens'}, dimensions={1} | all-to-all | bytes 5242880 | tf_op jit(solution)/shard_map/all_to_all | solution.py:55
  (255 shorter events, 1039.2 us)
Async XLA Ops:
  6.5 65.3 %all-gather.7.cloned.1.call-start = ((), (), s32[]{:S(2)}) async-start(), calls=%async_computation.14 | async-start | bytes 3932160 | tf_op jit(solution)/shard_map/all_gather | solution.py:13
  31.4 40.4 %copy-start.28 = (bf16[3,512,64]{1,2,0:T(8,128)(2,1)S(1)}, bf16[3,512,64]{1,2,0:T(8,128)(2,1)}, u32[]{:S(2)}) copy-start(bf16[3,512,64]{1,2,0:T(8,128)(2,1)} %param.15) | copy-start | bytes 589828
  32.7 119.9 %reduce-scatter.7.cloned.1.call-start = ((), (), s32[]{:S(2)}) async-start(), calls=%async_computation.15 | async-start | bytes 7864320 | tf_op jit(solution)/shard_map/reduce_scatter | solution.py:16
  89.5 63.1 %copy-start = (f32[4,5120,32]{1,2,0:T(8,128)S(1)}, f32[4,5120,32]{1,2,0:T(8,128)}, u32[]{:S(2)}) copy-start(f32[4,5120,32]{1,2,0:T(8,128)} %param.12) | copy-start | bytes 7864324
  89.5 123.9 %all-gather.9.cloned.1.call-start = ((), (), s32[]{:S(2)}) async-start(), calls=%async_computation.16 | async-start | bytes 3932160 | tf_op jit(solution)/shard_map/all_gather | solution.py:13
  177.1 117.0 %reduce-scatter.9.cloned.1.call-start = ((), (), s32[]{:S(2)}) async-start(), calls=%async_computation.17 | async-start | bytes 7864320 | tf_op jit(solution)/shard_map/reduce_scatter | solution.py:16
  231.1 124.7 %all-gather.11.cloned.1.call-start = ((), (), s32[]{:S(2)}) async-start(), calls=%async_computation.18 | async-start | bytes 3932160 | tf_op jit(solution)/shard_map/all_gather | solution.py:13
  319.6 117.0 %reduce-scatter.11.cloned.1.call-start = ((), (), s32[]{:S(2)}) async-start(), calls=%async_computation.19 | async-start | bytes 7864320 | tf_op jit(solution)/shard_map/reduce_scatter | solution.py:16
  543.5 34.1 %all-to-all-start.1 = ((f32[2,1,327680]{2,1,0:T(1,128)}), f32[2,1,327680]{2,1,0:T(1,128)S(1)}, u32[]{:S(2)}, u32[]{:S(2)}) async-start(f32[2,1,327680]{2,1,0:T(1,128)} %reshape.123), calls=%async_computation.4 | async-start | bytes 5242880 | tf_op jit(solution)/shard_map/all_to_all | solution.py:51
  547.5 521.2 %all-gather.13.cloned.1.call-start = ((), (), s32[]{:S(2)}) async-start(), calls=%async_computation.20 | async-start | bytes 3932160 | tf_op jit(solution)/shard_map/all_gather | solution.py:13
  548.2 94.9 %copy-start.19 = (pred[16,16]{1,0:T(8,128)(4,1)}, pred[16,16]{1,0:T(8,128)(4,1)S(1)}, u32[]{:S(2)}) copy-start(pred[16,16]{1,0:T(8,128)(4,1)S(1)} %iota_compare_fusion) | copy-start | bytes 772
  548.3 80.0 %copy-start.21 = (s32[1024]{0:T(1024)}, s32[1024]{0:T(1024)S(1)}, u32[]{:S(2)}) copy-start(s32[1024]{0:T(1024)S(1)} %pad_clamp_fusion) | copy-start | bytes 12292
  548.3 125.5 %copy-start.17 = (f32[16,16]{1,0:T(8,128)}, f32[16,16]{1,0:T(8,128)S(1)}, u32[]{:S(2)}) copy-start(f32[16,16]{1,0:T(8,128)S(1)} %get-tuple-element.15) | copy-start | bytes 3076
  548.3 346.0 %copy-start.5 = (f32[16,16]{1,0:T(8,128)}, f32[16,16]{1,0:T(8,128)S(1)}, u32[]{:S(2)}) copy-start(f32[16,16]{1,0:T(8,128)S(1)} %get-tuple-element.16) | copy-start | bytes 3076
  548.3 82.3 %copy-start.22 = (pred[32]{0:T(512)(128)(4,1)}, pred[32]{0:T(512)(128)(4,1)S(1)}, u32[]{:S(2)}) copy-start(pred[32]{0:T(512)(128)(4,1)S(1)} %compare_and_fusion) | copy-start | bytes 100
  1009.3 59.3 %copy-start.29 = (bf16[3,512,64]{1,2,0:T(8,128)(2,1)S(1)}, bf16[3,512,64]{1,2,0:T(8,128)(2,1)}, u32[]{:S(2)}) copy-start(bf16[3,512,64]{1,2,0:T(8,128)(2,1)} %param.15) | copy-start | bytes 589828
  1009.3 59.3 %copy-start.31 = (bf16[3,64,512]{2,1,0:T(8,128)(2,1)S(1)}, bf16[3,64,512]{2,1,0:T(8,128)(2,1)}, u32[]{:S(2)}) copy-start(bf16[3,64,512]{2,1,0:T(8,128)(2,1)} %param.14) | copy-start | bytes 589828
  1033.5 115.9 %reduce-scatter.13.cloned.1.call-start = ((), (), s32[]{:S(2)}) async-start(), calls=%async_computation.21 | async-start | bytes 7864320 | tf_op jit(solution)/shard_map/reduce_scatter | solution.py:16
  1086.4 127.6 %all-gather.15.cloned.1.call-start = ((), (), s32[]{:S(2)}) async-start(), calls=%async_computation.22 | async-start | bytes 3932160 | tf_op jit(solution)/shard_map/all_gather | solution.py:13
  1177.6 117.0 %reduce-scatter.15.cloned.1.call-start = ((), (), s32[]{:S(2)}) async-start(), calls=%async_computation.23 | async-start | bytes 7864320 | tf_op jit(solution)/shard_map/reduce_scatter | solution.py:16
  1231.6 63.1 %copy-start.1 = (f32[5120,4,32]{0,2,1:T(8,128)S(1)}, f32[5120,4,32]{0,2,1:T(8,128)}, u32[]{:S(2)}) copy-start(f32[5120,4,32]{0,2,1:T(8,128)} %add.141) | copy-start | bytes 7864324
  1231.6 127.6 %all-gather.17.cloned.1.call-start = ((), (), s32[]{:S(2)}) async-start(), calls=%async_computation.24 | async-start | bytes 3932160 | tf_op jit(solution)/shard_map/all_gather | solution.py:13
  1322.9 117.0 %reduce-scatter.17.cloned.1.call-start = ((), (), s32[]{:S(2)}) async-start(), calls=%async_computation.25 | async-start | bytes 7864320 | tf_op jit(solution)/shard_map/reduce_scatter | solution.py:16
  1376.9 63.1 %copy-start.2 = (f32[5120,4,32]{0,2,1:T(8,128)S(1)}, f32[5120,4,32]{0,2,1:T(8,128)}, u32[]{:S(2)}) copy-start(f32[5120,4,32]{0,2,1:T(8,128)} %add.144) | copy-start | bytes 7864324
  (26 other events, 337.7 us)
Sparse Core Ops, SparseCore 0:
  32.8 38.9 all-gather.6
  89.7 62.8 reduce-scatter.6
  177.3 36.1 all-gather.8
  231.3 62.8 reduce-scatter.8
  319.7 36.1 all-gather.10
  373.7 62.8 reduce-scatter.10
  1033.6 35.0 all-gather.12
  1086.5 62.8 reduce-scatter.12
  1177.8 36.1 all-gather.14
  1231.8 62.8 reduce-scatter.14
  1323.1 36.1 all-gather.16
  1377.1 62.8 reduce-scatter.16
where the time goes:
time: 2030 us; the launch traced here: 2020 us
  matrix products  826 us (41%)
  waiting for transfers between devices  626 us (31%)
  blocking collectives  238 us (12%)
  local copies, waits for them, and re-layouts  235 us (12%)
  other arithmetic  72.8 us (4%)
    reduce_scatter x6, waiting for transfers between devices, value_a8(): lax.psum_scatter(part_sum, 'model', scatter_dimension=2, tiled=True)  378 us
    all_gather x6, waiting for transfers between devices, value_a8(): mix_full = lax.all_gather(mix_out, 'model', axis=2, tiled=True)  219 us
    dot_general x22, matrix products, letkf_weights(): z_mat = jnp.matmul(t_mat, z_mat, precision=FULL_PREC)  159 us
    dot_general x22, matrix products, letkf_weights(): t_mat = 1.5 * identity - 0.5 * jnp.matmul(z_mat, b_mat, precision=FULL_PREC)  152 us
    dot_general x22, matrix products, letkf_weights(): b_mat = jnp.matmul(b_mat, t_mat, precision=FULL_PREC)  152 us
    dot_general x5, matrix products, value_a8(): jnp.einsum('ij,jkc->ikc', mix_op, ens_state.astype(jnp.bfloat16), preferr...  123 us
    dot_general x6, matrix products, value_a8(): jnp.einsum('ikf,fv->ikv', hidden.astype(jnp.bfloat16), w_out[layer_idx],...  106 us
    unnamed x82, local copies, waits for them, and re-layouts  85.6 us
  transfers between devices with their start and end apart: 13, of which 13 were waited for; matrix products, arithmetic and copies ran while one was open for 0% of the time, Pallas kernels for 0%

commit v1 on v0

v1 whole, which is shorter than its diff:
```python
import functools
import math

import jax
import jax.numpy as jnp
from jax import lax
from jax.experimental import pallas as pl
from jax.experimental.pallas import tpu as pltpu
from jax.sharding import PartitionSpec as P

MESH = pl.DeviceIdType.MESH
K = 16
COLS = 5120
VARS = 64
HID = 1024
BLK = 640
LANE = 128
TILES = 5
ROWS = 512
HALF = 2560
NS_STEPS = 12
VMEM_LIMIT = 64 * 1024 * 1024 - 64 * 1024
F32 = jnp.float32
BF16 = jnp.bfloat16
C0 = math.sqrt(2.0 / math.pi)
C1 = 2.0 * C0
C2 = 8.0 * 0.044715 * C0


def coords():
    e = lax.axis_index("ens")
    return e // 2, lax.axis_index("model"), e % 2


def dev(x, y, c):
    return {"model": y, "ens": 2 * x + c}


def greet():
    x, y, c = coords()
    barrier = pltpu.get_barrier_semaphore()
    for r in range(1, 8):
        dx, dy, dc = r // 4, (r // 2) % 2, r % 2
        pl.semaphore_signal(barrier, inc=1, device_id=dev((x + dx) % 2, (y + dy) % 2, (c + dc) % 2), device_id_type=MESH)
    pl.semaphore_wait(barrier, 7)


def await_bytes(ref, sem):
    pltpu.make_async_copy(ref, ref, sem).wait()


def gather_kernel(ens_ref, w_ref, u_ref, out_ref, wall_ref, uall_ref, send, recv, wsend, wrecv, wloc):
    x, y, c = coords()
    greet()
    v0 = pl.multiple_of(32 * y, 32)

    def piece(h):
        return ens_ref.at[:, :, pl.ds(HALF * h, HALF)], out_ref.at[:, pl.ds(v0, 32), :]

    for h in range(2):
        src, dst = piece(h)
        own = jnp.logical_and(c == y, c == h)

        @pl.when(jnp.logical_not(own))
        def _():
            pltpu.make_async_remote_copy(src, dst, send.at[h], recv.at[y], device_id=dev(x, c, h), device_id_type=MESH).start()

        @pl.when(own)
        def _():
            pltpu.make_async_copy(src, dst, recv.at[y]).start()

    weights = ((w_ref, wall_ref), (u_ref, uall_ref))
    for n, (src, dst) in enumerate(weights):
        pltpu.make_async_remote_copy(src, dst.at[y], wsend.at[n], wrecv.at[n], device_id=dev(x, 1 - y, c), device_id_type=MESH).start()
        pltpu.make_async_copy(src, dst.at[y], wloc.at[n]).start()
    for n, (src, dst) in enumerate(weights):
        pltpu.make_async_copy(src, dst.at[y], wloc.at[n]).wait()
        pltpu.make_async_remote_copy(src, dst.at[1 - y], wsend.at[n], wrecv.at[n], device_id=dev(x, 1 - y, c), device_id_type=MESH).wait()
    for h in range(2):
        src, dst = piece(h)
        own = jnp.logical_and(c == y, c == h)

        @pl.when(jnp.logical_not(own))
        def _():
            pltpu.make_async_remote_copy(src, dst, send.at[h], recv.at[y], device_id=dev(x, c, h), device_id_type=MESH).wait_send()
    for s in range(2):
        await_bytes(out_ref.at[:, pl.ds(32 * s, 32), :], recv.at[s])


def gather_state(ens_t, w_in, w_out_t):
    vm = pl.BlockSpec(memory_space=pltpu.VMEM)
    hbm = pl.BlockSpec(memory_space=pl.ANY)
    dma = pltpu.SemaphoreType.DMA
    return pl.pallas_call(
        gather_kernel,
        out_shape=(
            jax.ShapeDtypeStruct((4, VARS, HALF), F32),
            jax.ShapeDtypeStruct((2,) + w_in.shape, BF16),
            jax.ShapeDtypeStruct((2,) + w_out_t.shape, BF16),
        ),
        in_specs=[vm, vm, vm],
        out_specs=(hbm, hbm, hbm),
        scratch_shapes=[dma((2,)), dma((2,)), dma((2,)), dma((2,)), dma((2,))],
        compiler_params=pltpu.CompilerParams(collective_id=1, has_side_effects=True, vmem_limit_bytes=16 * 1024 * 1024),
        name="gather_state",
    )(ens_t, w_in, w_out_t)


def forecast_kernel(layers, ht_ref, a_ref, w_ref, u_ref, out_ref, a_vm, hb, hf, mt, st, a_sem, xsend, xrecv, send, recv):
    x, y, c = coords()
    partner = dev(x, y, 1 - c)
    greet()

    def a_copy(t, q):
        row = pl.multiple_of((4 * c + q) * BLK + LANE * t, LANE)
        return pltpu.make_async_copy(a_ref.at[pl.ds(row, LANE), :], a_vm.at[t, pl.ds(LANE * q, LANE), :], a_sem.at[t, q])

    for t in range(TILES):
        for q in range(4):
            a_copy(t, q).start()

    def share(buf, t):
        lane = pl.multiple_of(LANE * t, LANE)
        piece = hb.at[buf, pl.ds(4 * c, 4), pl.ds(lane, LANE), :]
        return pltpu.make_async_remote_copy(piece, piece, xsend.at[buf, t], xrecv.at[buf, t], device_id=partner, device_id_type=MESH)

    for t in range(TILES):
        for q in range(4):
            part = ht_ref[:, BLK * q + LANE * t:BLK * q + LANE * (t + 1)].T
            hf[t, LANE * q:LANE * (q + 1), :] = part
            hb[0, 4 * c + q, LANE * t:LANE * (t + 1), :] = part.astype(BF16)
        share(0, t).start()

    def await_share(buf, t):
        lane = pl.multiple_of(LANE * t, LANE)
        await_bytes(hb.at[buf, pl.ds(4 * (1 - c), 4), pl.ds(lane, LANE), :], xrecv.at[buf, t])

    own_half = x == c
    mine = 4 * (2 * x + y)

    def ship(t, q):
        c2, y2 = q // 2, q % 2
        lane = pl.multiple_of(LANE * t, LANE)
        src = st.at[t, :, :, pl.ds(LANE * q, LANE)]
        dst = out_ref.at[pl.ds(mine, 4), :, pl.ds(lane, LANE)]
        is_self = jnp.logical_and(own_half, jnp.logical_and(c == c2, y == y2))
        rsem = recv.at[t, 2 * x + y]
        def local():
            return pltpu.make_async_copy(src, dst, rsem)

        def remote():
            return pltpu.make_async_remote_copy(src, dst, send.at[t, q], rsem, device_id=dev(c, y2, c2), device_id_type=MESH)
        return is_self, local, remote

    def layer_body(layer, carry):
        cur = lax.rem(layer, 2)
        nxt = 1 - cur
        for t in range(TILES):
            await_share(cur, t)
            share(cur, t).wait_send()

        def tile_body(t, carry2):
            @pl.when(layer == 0)
            def _():
                for q in range(4):
                    a_copy(t, q).wait()
            state = hb[cur].reshape(COLS, 4 * VARS)
            mixed = jnp.dot(a_vm[t], state, preferred_element_type=F32)
            mt[...] = mixed.astype(BF16)
            for p in range(2):
                lhs = mt[:, 128 * p:128 * (p + 1)]
                total = None
                for n in range(8):
                    h = jnp.dot(lhs, w_ref[layer, :, 256 * n:256 * (n + 1)], preferred_element_type=F32)
                    z = h * (C1 + C2 * (h * h))
                    q_act = (h + h * jnp.tanh(z)).astype(BF16)
                    part = jnp.dot(q_act, u_ref[layer, 256 * n:256 * (n + 1), :], preferred_element_type=F32)
                    total = part if total is None else total + part
                hf[t, :, 128 * p:128 * (p + 1)] = hf[t, :, 128 * p:128 * (p + 1)] + total

            @pl.when(layer < layers - 1)
            def _():
                lane = pl.multiple_of(LANE * t, LANE)
                for q in range(4):
                    hb[nxt, 4 * c + q, pl.ds(lane, LANE), :] = hf[t, LANE * q:LANE * (q + 1), :].astype(BF16)
                share(nxt, t).start()

            @pl.when(layer == layers - 1)
            def _():
                for q in range(4):
                    st[t, :, :, LANE * q:LANE * (q + 1)] = hf[t, LANE * q:LANE * (q + 1), :].T.reshape(4, VARS, LANE)
                for q in range(4):
                    is_self, local, remote = ship(t, q)

                    @pl.when(is_self)
                    def _():
                        local().start()

                    @pl.when(jnp.logical_not(is_self))
                    def _():
                        remote().start()
            return carry2

        return lax.fori_loop(0, TILES, tile_body, carry)

    lax.fori_loop(0, layers, layer_body, 0)

    for t in range(TILES):
        for q in range(4):
            is_self, local, remote = ship(t, q)

            @pl.when(jnp.logical_not(is_self))
            def _():
                remote().wait_send()
    for t in range(TILES):
        for s in range(4):
            await_bytes(out_ref.at[4 * s:4 * s + 4, :, LANE * t:LANE * (t + 1)], recv.at[t, s])


def forecast(ht, mix_op, w_pair, u_pair):
    vm = pl.BlockSpec(memory_space=pltpu.VMEM)
    hbm = pl.BlockSpec(memory_space=pl.ANY)
    dma = pltpu.SemaphoreType.DMA
    layers = w_pair.shape[0]
    return pl.pallas_call(
        functools.partial(forecast_kernel, layers),
        out_shape=jax.ShapeDtypeStruct((K, VARS, BLK), F32),
        in_specs=[vm, hbm, vm, vm],
        out_specs=hbm,
        scratch_shapes=[
            pltpu.VMEM((TILES, ROWS, COLS), BF16),
            pltpu.VMEM((2, 8, BLK, 4 * VARS), BF16),
            pltpu.VMEM((TILES, ROWS, 4 * VARS), F32),
            pltpu.VMEM((ROWS, 4 * VARS), BF16),
            pltpu.VMEM((TILES, 4, VARS, ROWS), F32),
            dma((TILES, 4)),
            dma((2, TILES)),
            dma((2, TILES)),
            dma((TILES, 4)),
            dma((TILES, 4)),
        ],
        compiler_params=pltpu.CompilerParams(collective_id=2, has_side_effects=True, vmem_limit_bytes=VMEM_LIMIT),
        name="forecast",
    )(ht, mix_op, w_pair, u_pair)


def bcast(ref, row):
    return ref[pl.ds(row, 8, stride=0), :]


def right_factor(ref):
    top = [(ref[16 * k:16 * k + 8, :], ref[16 * k + 8:16 * k + 16, :]) for k in range(8)]
    low = [(ref[pl.ds(8 + a, 8, stride=16), :], ref[16 * (8 + a) + 8:16 * (8 + a) + 16, :]) for a in range(8)]
    return top + low


def sym_row(i, k):
    return 16 * k + i if (i >= 8 and k < 8) else 16 * i + k


def sym_product(left, right, emit):
    cols = right_factor(right)
    for i in range(16):
        lo = hi = None
        for k in range(16):
            s = bcast(left, sym_row(i, k))
            if i < 8:
                lo = s * cols[k][0] if lo is None else lo + s * cols[k][0]
            hi = s * cols[k][1] if hi is None else hi + s * cols[k][1]
        emit(i, lo, hi)


def analyse_tile(xin, t, idx_ref, yo_ref, ri_ref, rho, ob, xa, mref, yo, gp, bm, zm, tm, wa, st, write):
    lanes = pl.ds(pl.multiple_of(LANE * t, LANE), LANE)
    sub = lax.broadcasted_iota(jnp.int32, (8, LANE), 0)
    for v in range(8):
        rows = slice(8 * v, 8 * v + 8)
        vals = [xin[k, rows, lanes] for k in range(K)]
        total = vals[0]
        for k in range(1, K):
            total = total + vals[k]
        mean = total * (1.0 / K)
        mref[rows, :] = mean
        for k in range(K):
            xa[VARS * k + 8 * v:VARS * k + 8 * v + 8, :] = vals[k] - mean

    ob[0:32, :] = yo_ref[:, lanes]
    ob[32:64, :] = ri_ref[:, lanes]
    for p in range(32):
        col = idx_ref[p]
        y_lo = xa[pl.ds(col, 8, stride=VARS), :]
        y_hi = xa[pl.ds(col + 8 * VARS, 8, stride=VARS), :]
        prec = bcast(ob, 32 + p)
        yo[16 * p:16 * p + 8, :] = y_lo
        yo[16 * p + 8:16 * p + 16, :] = y_hi
        gp[16 * p:16 * p + 8, :] = y_lo * prec
        gp[16 * p + 8:16 * p + 16, :] = y_hi * prec
    g_lo = jnp.zeros((8, LANE), F32)
    g_hi = jnp.zeros((8, LANE), F32)
    for p in range(32):
        inno = bcast(ob, p) - bcast(mref, idx_ref[p])
        g_lo = g_lo + gp[16 * p:16 * p + 8, :] * inno
        g_hi = g_hi + gp[16 * p + 8:16 * p + 16, :] * inno
    diag = (K - 1) / rho
    trace = jnp.zeros((8, LANE), F32)
    for half in range(2):
        acc = [None] * 8
        acc2 = [None] * 8
        for p in range(32):
            y_lo = yo[16 * p:16 * p + 8, :]
            y_hi = yo[16 * p + 8:16 * p + 16, :]
            for r in range(8):
                s = bcast(gp, 16 * p + 8 * half + r)
                if half == 0:
                    acc[r] = s * y_lo if acc[r] is None else acc[r] + s * y_lo
                acc2[r] = s * y_hi if acc2[r] is None else acc2[r] + s * y_hi
        for r in range(8):
            i = 8 * half + r
            on = sub == r
            if half == 0:
                d = jnp.where(on, acc[r] + diag, acc[r])
                trace = trace + jnp.where(on, d, 0.0)
                bm[0, 16 * i:16 * i + 8, :] = d
                bm[0, 16 * i + 8:16 * i + 16, :] = acc2[r]
            else:
                d = jnp.where(on, acc2[r] + diag, acc2[r])
                trace = trace + jnp.where(on, d, 0.0)
                bm[0, 16 * i + 8:16 * i + 16, :] = d
    trace = jnp.broadcast_to(jnp.sum(trace, axis=0, keepdims=True), (8, LANE))
    inv = 1.0 / trace

    def slots(i):
        out = [(16 * i + 8, i >= 8)]
        if i < 8:
            out.append((16 * i, True))
        return out

    for i in range(16):
        for row, has_diag in slots(i):
            b = bm[0, row:row + 8, :] * inv
            bm[0, row:row + 8, :] = b
            z = b * -0.5
            if has_diag:
                z = jnp.where(sub == i % 8, z + 1.5, z)
            tm[row:row + 8, :] = z
            zm[0, row:row + 8, :] = z

    def emit_to(ref):
        def emit(i, lo, hi):
            if lo is not None:
                ref[16 * i:16 * i + 8, :] = lo
            ref[16 * i + 8:16 * i + 16, :] = hi
        return emit

    def emit_t(i, lo, hi):
        hi = hi * -0.5
        if lo is not None:
            lo = lo * -0.5
            tm[16 * i:16 * i + 8, :] = jnp.where(sub == i % 8, lo + 1.5, lo)
        else:
            hi = jnp.where(sub == i % 8, hi + 1.5, hi)
        tm[16 * i + 8:16 * i + 16, :] = hi

    def ns_step(step, carry):
        cur = lax.rem(step, 2)
        nxt = 1 - cur
        b_cur, b_nxt = bm.at[cur], bm.at[nxt]
        z_cur, z_nxt = zm.at[cur], zm.at[nxt]
        sym_product(b_cur, tm, emit_to(b_nxt))
        sym_product(z_cur, b_nxt, emit_t)
        sym_product(tm, z_cur, emit_to(z_nxt))
        return carry

    lax.fori_loop(0, NS_STEPS - 1, ns_step, 0)
    last = (NS_STEPS - 1) % 2
    z_fin = zm.at[last]

    root = 1.0 / jnp.sqrt(trace)
    cols = [(lo * root, hi * root) for lo, hi in right_factor(z_fin)]

    def sym_apply(lo, hi):
        gp[0:8, :] = lo
        gp[8:16, :] = hi
        a = b = None
        for k in range(16):
            s = bcast(gp, k)
            a = s * cols[k][0] if a is None else a + s * cols[k][0]
            b = s * cols[k][1] if b is None else b + s * cols[k][1]
        return a, b

    h_lo, h_hi = sym_apply(g_lo, g_hi)
    w_lo, w_hi = sym_apply(h_lo, h_hi)
    gp[0:8, :] = w_lo
    gp[8:16, :] = w_hi
    scale = math.sqrt(K - 1)
    for i in range(16):
        w = bcast(gp, i)
        wa[16 * i:16 * i + 8, :] = cols[i][0] * scale + w
        wa[16 * i + 8:16 * i + 16, :] = cols[i][1] * scale + w

    for v in range(0, 8, 2):
        xs = [(xa[VARS * i + 8 * v:VARS * i + 8 * v + 8, :], xa[VARS * i + 8 * v + 8:VARS * i + 8 * v + 16, :]) for i in range(K)]
        for k in range(K):
            a = mref[8 * v:8 * v + 8, :]
            b = mref[8 * v + 8:8 * v + 16, :]
            for i in range(K):
                s = bcast(wa, 16 * i + k)
                a = a + s * xs[i][0]
                b = b + s * xs[i][1]
            write(k, 8 * v, a, b)


def analysis_kernel(final, xin, idx_ref, yo_ref, ri_ref, rho_ref, out_ref, ob, xa, mref, yo, gp, bm, zm, tm, wa, st, send, recv):
    x, y, c = coords()
    greet()
    block = 4 * x + 2 * c + y

    if final:
        targets = [(r // 4, (r // 2) % 2, r % 2) for r in range(7, -1, -1)]
    else:
        targets = [(1, 1), (1, 0), (0, 1), (0, 0)]

    def ship(t, n):
        if final:
            dx, dy, dc = targets[n]
            x2, y2, c2 = (x + dx) % 2, (y + dy) % 2, (c + dc) % 2
            lane = pl.multiple_of(block * BLK + LANE * t, LANE)
            src = st.at[t, pl.ds(4 * (2 * x2 + c2), 4), pl.ds(pl.multiple_of(32 * y2, 32), 32), :]
            dst = out_ref.at[:, :, pl.ds(lane, LANE)]
            rsem = recv.at[t, block]
            is_self = n == len(targets) - 1
        else:
            dx, dy = targets[n]
            x2, y2, c2 = (x + dx) % 2, (y + dy) % 2, x
            lane = pl.multiple_of((2 * c + y) * BLK + LANE * t, LANE)
            src = st.at[t, pl.ds(4 * (2 * x2 + y2), 4), :, :]
            dst = out_ref.at[:, :, pl.ds(lane, LANE)]
            rsem = recv.at[t, 2 * c + y]
            is_self = (x == c) if n == len(targets) - 1 else False
        def local():
            return pltpu.make_async_copy(src, dst, rsem)

        def remote():
            return pltpu.make_async_remote_copy(src, dst, send.at[t, n], rsem, device_id=dev(x2, y2, c2), device_id_type=MESH)
        return is_self, local, remote

    def either(flag, yes, no):
        if flag is True:
            yes()
        elif flag is False:
            no()
        else:
            pl.when(flag)(yes)
            pl.when(jnp.logical_not(flag))(no)

    def tile(t, carry):
        def write(k, row, a, b):
            st[t, k, row:row + 8, :] = a
            st[t, k, row + 8:row + 16, :] = b
        analyse_tile(xin, t, idx_ref, yo_ref, ri_ref, rho_ref[0], ob, xa, mref, yo, gp, bm, zm, tm, wa, st, write)
        for n in range(len(targets)):
            is_self, local, remote = ship(t, n)
            either(is_self, lambda: local().start(), lambda: remote().start())
        return carry

    lax.fori_loop(0, TILES, tile, 0)
    for t in range(TILES):
        for n in range(len(targets)):
            is_self, local, remote = ship(t, n)
            either(is_self, lambda: None, lambda: remote().wait_send())
    for t in range(TILES):
        for s in range(8 if final else 4):
            lo = BLK * s + LANE * t
            await_bytes(out_ref.at[:, :, lo:lo + LANE], recv.at[t, s])


def analysis(state, obs_idx, obs_t, prec_t, rho, final):
    vm = pl.BlockSpec(memory_space=pltpu.VMEM)
    sm = pl.BlockSpec(memory_space=pltpu.SMEM)
    hbm = pl.BlockSpec(memory_space=pl.ANY)
    dma = pltpu.SemaphoreType.DMA
    out = (4, 32, COLS) if final else (4, VARS, HALF)
    peers = 8 if final else 4
    return pl.pallas_call(
        functools.partial(analysis_kernel, final),
        out_shape=jax.ShapeDtypeStruct(out, F32),
        in_specs=[vm, sm, vm, vm, sm],
        out_specs=hbm,
        scratch_shapes=[
            pltpu.VMEM((64, LANE), F32),
            pltpu.VMEM((K * VARS, LANE), F32),
            pltpu.VMEM((VARS, LANE), F32),
            pltpu.VMEM((512, LANE), F32),
            pltpu.VMEM((512, LANE), F32),
            pltpu.VMEM((2, 256, LANE), F32),
            pltpu.VMEM((2, 256, LANE), F32),
            pltpu.VMEM((256, LANE), F32),
            pltpu.VMEM((256, LANE), F32),
            pltpu.VMEM((TILES, K, VARS, LANE), F32),
            dma((TILES, peers)),
            dma((TILES, peers)),
        ],
        compiler_params=pltpu.CompilerParams(collective_id=4 if final else 3, has_side_effects=True, vmem_limit_bytes=32 * 1024 * 1024),
        name="analysis_last" if final else "analysis",
    )(state, obs_idx, obs_t, prec_t, rho)


def solution(mesh):
    def local_step(ens_local, mix_op, w_in, w_out, obs_val, obs_prec, obs_idx, inflation):
        cycles = obs_val.shape[0]
        ens_t = jnp.transpose(ens_local, (0, 2, 1))
        w_out_t = jnp.transpose(w_out, (0, 2, 1))
        obs_t = jnp.transpose(obs_val, (0, 2, 1))
        prec_t = jnp.transpose(obs_prec, (1, 0))
        ht, w_all, u_all = gather_state(ens_t, w_in, w_out_t)
        w_half = jnp.concatenate([w_all[0], w_all[1]], axis=2) * 0.5
        u_full = jnp.concatenate([u_all[0], u_all[1]], axis=2)
        w_pair = jnp.concatenate([jnp.pad(w_half, ((0, 0), (0, VARS), (0, 0))), jnp.pad(w_half, ((0, 0), (VARS, 0), (0, 0)))], axis=2)
        u_pair = jnp.concatenate([jnp.pad(u_full, ((0, 0), (0, VARS), (0, 0))), jnp.pad(u_full, ((0, 0), (VARS, 0), (0, 0)))], axis=2)
        u_pair = jnp.transpose(u_pair, (0, 2, 1))
        for cycle in range(cycles):
            final = cycle == cycles - 1
            state = forecast(ht.reshape(4 * VARS, HALF), mix_op, w_pair, u_pair)
            ht = analysis(state, obs_idx, obs_t[cycle], prec_t, inflation, final)
        return jnp.transpose(ht, (0, 2, 1))

    member_spec = P(("case", "ens"), None, "model")
    col_axes = ("case", "ens", "model")
    in_specs = (member_spec, P(None, None), P(None, None, "model"), P(None, "model", None), P(None, col_axes, None), P(col_axes, None), P(None), P(None))
    return jax.shard_map(local_step, mesh=mesh, in_specs=in_specs, out_specs=member_spec, check_vma=False)
```

time: 2030 us -> 378 us (0.19)
  matrix products: 826 us -> 0 us
  waiting for transfers between devices: 626 us -> 0 us
  Pallas kernels: 0 us -> 355 us
  blocking collectives: 238 us -> 0 us
  local copies, waits for them, and re-layouts: 235 us -> 18.5 us
  other arithmetic: 72.8 us -> 3.18 us
    dot_general x87 -> x0, matrix products: 803 us -> none  [the longest x22 159 us: letkf_weights(): z_mat = jnp.matmul(t_mat, z_mat, precision=FULL_PREC)]
    reduce_scatter x6 -> x0, waiting for transfers between devices: 378 us -> none  [value_a8(): lax.psum_scatter(part_sum, 'model', scatter_dimension=2, tiled=True)]
    pallas_call x0 -> x5, Pallas kernels: none -> 355 us  [the longest x2 232 us: forecast(): pl.pallas_call(functools.partial(forecast_kernel, layers), out_shape=jax....]
    all_to_all x7 -> x0, blocking collectives: 238 us -> none  [the longest x2 70.2 us: local_step(): col_state = lax.all_to_all(ens_state, 'ens', 0, 1, tiled=True)]
    all_gather x6 -> x0, waiting for transfers between devices: 219 us -> none  [value_a8(): mix_full = lax.all_gather(mix_out, 'model', axis=2, tiled=True)]
    all_to_all x17 -> x0, local copies, waits for them, and re-layouts: 76.4 us -> none  [the longest x6 33.3 us: local_step(): col_state = lax.all_to_all(col_state, 'model', 0, 2, tiled=True)]
    unnamed x82 -> x27, local copies, waits for them, and re-layouts: 85.6 us -> 16.4 us
    all_to_all x4 -> x0, other arithmetic: 38.9 us -> none  [the longest x2 20.3 us: local_step(): col_state = lax.all_to_all(col_state, 'model', 0, 2, tiled=True)]
  transfers between devices with their start and end apart: 13 -> 0, of which waited for: 13 -> 0; matrix products, arithmetic and copies ran while one was open for 0% -> 0% of each run, Pallas kernels for 0% -> 0%
where the time goes in v1:
time: 378 us; the launch traced here: 377 us
  Pallas kernels  355 us (94%)
  local copies, waits for them, and re-layouts  18.5 us (5%)
    pallas_call x2, Pallas kernels, forecast(): pl.pallas_call(functools.partial(forecast_kernel, layers), out_shape=jax....  232 us
    pallas_call x2, Pallas kernels, analysis(): pl.pallas_call(functools.partial(analysis_kernel, final), out_shape=jax.S...  80.5 us
    pallas_call x1, Pallas kernels, gather_state(): pl.pallas_call(gather_kernel, out_shape=(jax.ShapeDtypeStruct((4, VARS, H...  42.5 us
    unnamed x27, local copies, waits for them, and re-layouts  16.4 us

profile of v1, /device:TPU:0, one launch (start us, length us, event | category | flops | bytes accessed | tf_op | source)
XLA Modules:
  0.0 377.4 jit_solution(7337199427816811732)
XLA Ops:
  0.7 1.6 slice_bitcast_fusion.4
  2.3 1.7 copy-done.3
  4.0 0.9 copy-done.9
  4.9 0.9 copy-done.10
  5.9 42.5 %gather_state.1 = (f32[4,64,2560]{2,1,0:T(8,128)S(1)}, bf16[2,3,64,512]{3,2,1,0:T(8,128)(2,1)S(1)}, bf16[2,3,64,512]{3,2,1,0:T(8,128)(2,1)S(1)}) custom-call(f32[4,32,5120]{2,1,0:T(8,128)S(1)} %bitcast.23, bf16[3,64,512]{2,1,0:T(8,128)(2,1)S(1)} %copy-done.9, bf16[3,64,512]{2,1,0:T(8,128)(2,1)S(1)} %bitcast.27), custom_call_target="tpu_custom_call" | custom-call | tf_op jit(solution)/shard_map/gather_state/pallas_call | solution.py:94
  48.4 1.5 copy-done.4
  50.0 0.4 copy.9
  50.5 0.2 pad_maximum_fusion
  50.6 1.6 fusion.5.u_ref
  52.2 1.4 fusion.6.w_ref
  53.6 115.6 %forecast.2.xin = f32[16,64,640]{2,1,0:T(8,128)} custom-call(f32[256,2560]{1,0:T(8,128)} %bitcast.24, bf16[5120,5120]{1,0:T(8,128)(2,1)} %a_ref.3, bf16[3,128,2048]{2,1,0:T(8,128)(2,1)} %fusion.6.w_ref, bf16[3,2048,128]{2,1,0:T(8,128)(2,1)} %fusion.5.u_ref), custom_call_target="tpu_custom_call" | custom-call | tf_op jit(solution)/shard_map/forecast/pallas_call | solution.py:225
  169.2 1.7 copy-done.2
  170.9 0.9 copy-done.6
  171.8 0.9 copy-done.7
  172.7 0.7 copy-done.11
  173.3 39.9 %analysis.1 = f32[4,64,2560]{2,1,0:T(8,128)S(1)} custom-call(f32[16,64,640]{2,1,0:T(8,128)S(1)} %copy-done.2, s32[32]{0:T(128)S(1)} %copy-done.11, f32[32,640]{1,0:T(8,128)S(1)} %copy-done.6, f32[32,640]{1,0:T(8,128)S(1)} %bitcast.25, f32[1]{0:T(128)S(6)} %copy.12.rho_ref), custom_call_target="tpu_custom_call" | custom-call | tf_op jit(solution)/shard_map/analysis/pallas_call | solution.py:484
  213.3 1.5 copy-done.1
  214.7 116.3 %forecast.3.xin = f32[16,64,640]{2,1,0:T(8,128)} custom-call(f32[256,2560]{1,0:T(8,128)} %bitcast.22, bf16[5120,5120]{1,0:T(8,128)(2,1)} %a_ref.3, bf16[3,128,2048]{2,1,0:T(8,128)(2,1)} %fusion.6.w_ref, bf16[3,2048,128]{2,1,0:T(8,128)(2,1)} %fusion.5.u_ref), custom_call_target="tpu_custom_call" | custom-call | tf_op jit(solution)/shard_map/forecast/pallas_call | solution.py:225
  331.1 1.7 copy-done
  332.8 0.9 copy-done.5
  333.7 0.9 copy-done.8
  334.6 0.7 copy-done.12
  335.3 40.6 %analysis_last.1 = f32[4,32,5120]{2,1,0:T(8,128)S(1)} custom-call(f32[16,64,640]{2,1,0:T(8,128)S(1)} %copy-done, s32[32]{0:T(128)S(1)} %copy-done.12, f32[32,640]{1,0:T(8,128)S(1)} %copy-done.5, f32[32,640]{1,0:T(8,128)S(1)} %bitcast.26, f32[1]{0:T(128)S(6)} %copy.12.rho_ref), custom_call_target="tpu_custom_call" | custom-call | tf_op jit(solution)/shard_map/analysis_last/pallas_call | solution.py:484
  375.9 1.5 copy.13
  (16 shorter events, 0.2 us)
Async XLA Ops:
  2.3 1.7 copy-start.3
  4.0 0.9 copy-start.9
  4.9 0.9 copy-start.10
  48.4 1.5 copy-start.4
  169.2 1.7 copy-start.2
  170.9 0.9 copy-start.6
  171.8 0.9 copy-start.7
  172.7 0.7 copy-start.11
  213.2 1.5 copy-start.1
  331.1 1.7 copy-start
  332.8 0.9 copy-start.5
  333.7 0.9 copy-start.8
  334.6 0.7 copy-start.12

commit v2 on v1

--- a/solution.py
+++ b/solution.py
@@ -165,18 +165,19 @@
                 for q in range(4):
                     a_copy(t, q).wait()
             state = hb[cur].reshape(COLS, 4 * VARS)
-            mixed = jnp.dot(a_vm[t], state, preferred_element_type=F32)
-            mt[...] = mixed.astype(BF16)
-            for p in range(2):
-                lhs = mt[:, 128 * p:128 * (p + 1)]
-                total = None
-                for n in range(8):
-                    h = jnp.dot(lhs, w_ref[layer, :, 256 * n:256 * (n + 1)], preferred_element_type=F32)
+            for r in range(2):
+                mixed = jnp.dot(a_vm[t, 256 * r:256 * (r + 1), :], state, preferred_element_type=F32)
+                mt[256 * r:256 * (r + 1), :] = mixed.astype(BF16)
+            sums = [None, None]
+            for n in range(8):
+                for p in range(2):
+                    h = jnp.dot(mt[:, 128 * p:128 * (p + 1)], w_ref[layer, :, 256 * n:256 * (n + 1)], preferred_element_type=F32)
                     z = h * (C1 + C2 * (h * h))
                     q_act = (h + h * jnp.tanh(z)).astype(BF16)
                     part = jnp.dot(q_act, u_ref[layer, 256 * n:256 * (n + 1), :], preferred_element_type=F32)
-                    total = part if total is None else total + part
-                hf[t, :, 128 * p:128 * (p + 1)] = hf[t, :, 128 * p:128 * (p + 1)] + total
+                    sums[p] = part if sums[p] is None else sums[p] + part
+            for p in range(2):
+                hf[t, :, 128 * p:128 * (p + 1)] = hf[t, :, 128 * p:128 * (p + 1)] + sums[p]
 
             @pl.when(layer < layers - 1)
             def _():

time: 378 us -> 316 us (0.84)
  Pallas kernels: 355 us -> 293 us
    pallas_call x2, Pallas kernels: 232 us -> 170 us  [forecast(): pl.pallas_call(functools.partial(forecast_kernel, layers), out_shape=jax....]
where the time goes in v2:
time: 316 us; the launch traced here: 315 us
  Pallas kernels  293 us (93%)
  local copies, waits for them, and re-layouts  18.5 us (6%)
  other arithmetic  3.18 us (1%)
    pallas_call x2, Pallas kernels, forecast(): pl.pallas_call(functools.partial(forecast_kernel, layers), out_shape=jax....  170 us
    pallas_call x2, Pallas kernels, analysis(): pl.pallas_call(functools.partial(analysis_kernel, final), out_shape=jax.S...  80.5 us
    pallas_call x1, Pallas kernels, gather_state(): pl.pallas_call(gather_kernel, out_shape=(jax.ShapeDtypeStruct((4, VARS, H...  42.5 us
    unnamed x27, local copies, waits for them, and re-layouts  16.4 us

profile of v2, /device:TPU:0, one launch (start us, length us, event | category | flops | bytes accessed | tf_op | source)
XLA Modules:
  0.0 315.1 jit_solution(6527748118376326286)
XLA Ops:
  0.7 1.6 slice_bitcast_fusion.4
  2.3 1.7 copy-done.3
  4.0 0.9 copy-done.9
  4.9 0.9 copy-done.10
  5.9 42.5 %gather_state.1 = (f32[4,64,2560]{2,1,0:T(8,128)S(1)}, bf16[2,3,64,512]{3,2,1,0:T(8,128)(2,1)S(1)}, bf16[2,3,64,512]{3,2,1,0:T(8,128)(2,1)S(1)}) custom-call(f32[4,32,5120]{2,1,0:T(8,128)S(1)} %bitcast.23, bf16[3,64,512]{2,1,0:T(8,128)(2,1)S(1)} %copy-done.9, bf16[3,64,512]{2,1,0:T(8,128)(2,1)S(1)} %bitcast.27), custom_call_target="tpu_custom_call" | custom-call | tf_op jit(solution)/shard_map/gather_state/pallas_call | solution.py:94
  48.4 1.5 copy-done.4
  50.0 0.4 copy.9
  50.5 0.2 pad_maximum_fusion
  50.6 1.6 fusion.5.u_ref
  52.2 1.4 fusion.6.w_ref
  53.6 84.4 %forecast.2.xin = f32[16,64,640]{2,1,0:T(8,128)} custom-call(f32[256,2560]{1,0:T(8,128)} %bitcast.24, bf16[5120,5120]{1,0:T(8,128)(2,1)} %a_ref.3, bf16[3,128,2048]{2,1,0:T(8,128)(2,1)} %fusion.6.w_ref, bf16[3,2048,128]{2,1,0:T(8,128)(2,1)} %fusion.5.u_ref), custom_call_target="tpu_custom_call" | custom-call | tf_op jit(solution)/shard_map/forecast/pallas_call | solution.py:226
  138.0 1.7 copy-done.2
  139.7 0.9 copy-done.6
  140.6 0.9 copy-done.7
  141.5 0.7 copy-done.11
  142.1 39.9 %analysis.1 = f32[4,64,2560]{2,1,0:T(8,128)S(1)} custom-call(f32[16,64,640]{2,1,0:T(8,128)S(1)} %copy-done.2, s32[32]{0:T(128)S(1)} %copy-done.11, f32[32,640]{1,0:T(8,128)S(1)} %copy-done.6, f32[32,640]{1,0:T(8,128)S(1)} %bitcast.25, f32[1]{0:T(128)S(6)} %copy.12.rho_ref), custom_call_target="tpu_custom_call" | custom-call | tf_op jit(solution)/shard_map/analysis/pallas_call | solution.py:485
  182.1 1.5 copy-done.1
  183.6 85.2 %forecast.3.xin = f32[16,64,640]{2,1,0:T(8,128)} custom-call(f32[256,2560]{1,0:T(8,128)} %bitcast.22, bf16[5120,5120]{1,0:T(8,128)(2,1)} %a_ref.3, bf16[3,128,2048]{2,1,0:T(8,128)(2,1)} %fusion.6.w_ref, bf16[3,2048,128]{2,1,0:T(8,128)(2,1)} %fusion.5.u_ref), custom_call_target="tpu_custom_call" | custom-call | tf_op jit(solution)/shard_map/forecast/pallas_call | solution.py:226
  268.8 1.7 copy-done
  270.5 0.9 copy-done.5
  271.4 0.9 copy-done.8
  272.3 0.7 copy-done.12
  273.0 40.6 %analysis_last.1 = f32[4,32,5120]{2,1,0:T(8,128)S(1)} custom-call(f32[16,64,640]{2,1,0:T(8,128)S(1)} %copy-done, s32[32]{0:T(128)S(1)} %copy-done.12, f32[32,640]{1,0:T(8,128)S(1)} %copy-done.5, f32[32,640]{1,0:T(8,128)S(1)} %bitcast.26, f32[1]{0:T(128)S(6)} %copy.12.rho_ref), custom_call_target="tpu_custom_call" | custom-call | tf_op jit(solution)/shard_map/analysis_last/pallas_call | solution.py:485
  313.6 1.5 copy.13
  (16 shorter events, 0.2 us)
Async XLA Ops:
  2.3 1.7 copy-start.3
  4.0 0.9 copy-start.9
  4.9 0.9 copy-start.10
  48.4 1.5 copy-start.4
  138.0 1.7 copy-start.2
  139.7 0.9 copy-start.6
  140.6 0.9 copy-start.7
  141.5 0.7 copy-start.11
  182.1 1.5 copy-start.1
  268.8 1.7 copy-start
  270.5 0.9 copy-start.5
  271.4 0.9 copy-start.8
  272.3 0.7 copy-start.12

commit v3 on v1

v3 whole, which is shorter than its diff:
```python
import functools
import math

import jax
import jax.numpy as jnp
from jax import lax
from jax.experimental import pallas as pl
from jax.experimental.pallas import tpu as pltpu
from jax.sharding import PartitionSpec as P

MESH = pl.DeviceIdType.MESH
K = 16
COLS = 5120
VARS = 64
HID = 1024
BLK = 640
LANE = 128
TILES = 5
ROWS = 512
HALF = 2560
NS_STEPS = 12
VMEM_LIMIT = 64 * 1024 * 1024 - 64 * 1024
F32 = jnp.float32
BF16 = jnp.bfloat16
C0 = math.sqrt(2.0 / math.pi)
C1 = 2.0 * C0
C2 = 8.0 * 0.044715 * C0


def coords():
    e = lax.axis_index("ens")
    return e // 2, lax.axis_index("model"), e % 2


def dev(x, y, c):
    return {"model": y, "ens": 2 * x + c}


def greet():
    x, y, c = coords()
    barrier = pltpu.get_barrier_semaphore()
    for r in range(1, 8):
        dx, dy, dc = r // 4, (r // 2) % 2, r % 2
        pl.semaphore_signal(barrier, inc=1, device_id=dev((x + dx) % 2, (y + dy) % 2, (c + dc) % 2), device_id_type=MESH)
    pl.semaphore_wait(barrier, 7)


def await_bytes(ref, sem):
    pltpu.make_async_copy(ref, ref, sem).wait()


def bcast(ref, row):
    return ref[pl.ds(row, 8, stride=0), :]


def right_factor(ref):
    top = [(ref[16 * k:16 * k + 8, :], ref[16 * k + 8:16 * k + 16, :]) for k in range(8)]
    low = [(ref[pl.ds(8 + a, 8, stride=16), :], ref[16 * (8 + a) + 8:16 * (8 + a) + 16, :]) for a in range(8)]
    return top + low


def sym_row(i, k):
    return 16 * k + i if (i >= 8 and k < 8) else 16 * i + k


def sym_product(left, right, emit):
    cols = right_factor(right)
    for i in range(16):
        lo = hi = None
        for k in range(16):
            s = bcast(left, sym_row(i, k))
            if i < 8:
                lo = s * cols[k][0] if lo is None else lo + s * cols[k][0]
            hi = s * cols[k][1] if hi is None else hi + s * cols[k][1]
        emit(i, lo, hi)


def analyse_tile(xin, t, idx_ref, yo_ref, ri_ref, rho, ob, xa, mref, yo, gp, bm, zm, tm, wa, write):
    lanes = pl.ds(pl.multiple_of(LANE * t, LANE), LANE)
    sub = lax.broadcasted_iota(jnp.int32, (8, LANE), 0)
    for v in range(8):
        rows = slice(8 * v, 8 * v + 8)
        vals = [xin[k, rows, lanes] for k in range(K)]
        total = vals[0]
        for k in range(1, K):
            total = total + vals[k]
        mean = total * (1.0 / K)
        mref[rows, :] = mean
        for k in range(K):
            xa[VARS * k + 8 * v:VARS * k + 8 * v + 8, :] = vals[k] - mean

    ob[0:32, :] = yo_ref[:, lanes]
    ob[32:64, :] = ri_ref[:, lanes]
    for p in range(32):
        col = idx_ref[p]
        y_lo = xa[pl.ds(col, 8, stride=VARS), :]
        y_hi = xa[pl.ds(col + 8 * VARS, 8, stride=VARS), :]
        prec = bcast(ob, 32 + p)
        yo[16 * p:16 * p + 8, :] = y_lo
        yo[16 * p + 8:16 * p + 16, :] = y_hi
        gp[16 * p:16 * p + 8, :] = y_lo * prec
        gp[16 * p + 8:16 * p + 16, :] = y_hi * prec
    g_lo = jnp.zeros((8, LANE), F32)
    g_hi = jnp.zeros((8, LANE), F32)
    for p in range(32):
        inno = bcast(ob, p) - bcast(mref, idx_ref[p])
        g_lo = g_lo + gp[16 * p:16 * p + 8, :] * inno
        g_hi = g_hi + gp[16 * p + 8:16 * p + 16, :] * inno
    diag = (K - 1) / rho
    trace = jnp.zeros((8, LANE), F32)
    for half in range(2):
        acc = [None] * 8
        acc2 = [None] * 8
        for p in range(32):
            y_lo = yo[16 * p:16 * p + 8, :]
            y_hi = yo[16 * p + 8:16 * p + 16, :]
            for r in range(8):
                s = bcast(gp, 16 * p + 8 * half + r)
                if half == 0:
                    acc[r] = s * y_lo if acc[r] is None else acc[r] + s * y_lo
                acc2[r] = s * y_hi if acc2[r] is None else acc2[r] + s * y_hi
        for r in range(8):
            i = 8 * half + r
            on = sub == r
            if half == 0:
                d = jnp.where(on, acc[r] + diag, acc[r])
                trace = trace + jnp.where(on, d, 0.0)
                bm[0, 16 * i:16 * i + 8, :] = d
                bm[0, 16 * i + 8:16 * i + 16, :] = acc2[r]
            else:
                d = jnp.where(on, acc2[r] + diag, acc2[r])
                trace = trace + jnp.where(on, d, 0.0)
                bm[0, 16 * i + 8:16 * i + 16, :] = d
    trace = jnp.broadcast_to(jnp.sum(trace, axis=0, keepdims=True), (8, LANE))
    inv = 1.0 / trace

    def slots(i):
        out = [(16 * i + 8, i >= 8)]
        if i < 8:
            out.append((16 * i, True))
        return out

    for i in range(16):
        for row, has_diag in slots(i):
            b = bm[0, row:row + 8, :] * inv
            bm[0, row:row + 8, :] = b
            z = b * -0.5
            if has_diag:
                z = jnp.where(sub == i % 8, z + 1.5, z)
            tm[row:row + 8, :] = z
            zm[0, row:row + 8, :] = z

    def emit_to(ref):
        def emit(i, lo, hi):
            if lo is not None:
                ref[16 * i:16 * i + 8, :] = lo
            ref[16 * i + 8:16 * i + 16, :] = hi
        return emit

    def emit_t(i, lo, hi):
        hi = hi * -0.5
        if lo is not None:
            lo = lo * -0.5
            tm[16 * i:16 * i + 8, :] = jnp.where(sub == i % 8, lo + 1.5, lo)
        else:
            hi = jnp.where(sub == i % 8, hi + 1.5, hi)
        tm[16 * i + 8:16 * i + 16, :] = hi

    def ns_step(step, carry):
        cur = lax.rem(step, 2)
        nxt = 1 - cur
        b_cur, b_nxt = bm.at[cur], bm.at[nxt]
        z_cur, z_nxt = zm.at[cur], zm.at[nxt]
        sym_product(b_cur, tm, emit_to(b_nxt))
        sym_product(z_cur, b_nxt, emit_t)
        sym_product(tm, z_cur, emit_to(z_nxt))
        return carry

    lax.fori_loop(0, NS_STEPS - 1, ns_step, 0)
    last = (NS_STEPS - 1) % 2
    z_fin = zm.at[last]

    root = 1.0 / jnp.sqrt(trace)
    cols = [(lo * root, hi * root) for lo, hi in right_factor(z_fin)]

    def sym_apply(lo, hi):
        gp[0:8, :] = lo
        gp[8:16, :] = hi
        a = b = None
        for k in range(16):
            s = bcast(gp, k)
            a = s * cols[k][0] if a is None else a + s * cols[k][0]
            b = s * cols[k][1] if b is None else b + s * cols[k][1]
        return a, b

    h_lo, h_hi = sym_apply(g_lo, g_hi)
    w_lo, w_hi = sym_apply(h_lo, h_hi)
    gp[0:8, :] = w_lo
    gp[8:16, :] = w_hi
    scale = math.sqrt(K - 1)
    for i in range(16):
        w = bcast(gp, i)
        wa[16 * i:16 * i + 8, :] = cols[i][0] * scale + w
        wa[16 * i + 8:16 * i + 16, :] = cols[i][1] * scale + w

    for v in range(0, 8, 2):
        xs = [(xa[VARS * i + 8 * v:VARS * i + 8 * v + 8, :], xa[VARS * i + 8 * v + 8:VARS * i + 8 * v + 16, :]) for i in range(K)]
        for k in range(K):
            a = mref[8 * v:8 * v + 8, :]
            b = mref[8 * v + 8:8 * v + 16, :]
            for i in range(K):
                s = bcast(wa, 16 * i + k)
                a = a + s * xs[i][0]
                b = b + s * xs[i][1]
            write(k, 8 * v, a, b)


def either(flag, yes, no):
    if flag is True:
        yes()
    elif flag is False:
        no()
    else:
        pl.when(flag)(yes)
        pl.when(jnp.logical_not(flag))(no)


def cycle_kernel(layers, cycles, ens_ref, win_ref, wout_ref, a_ref, obs_ref, prec_ref, idx_ref, rho_ref, out_ref,
                 a_vm, hb, hf, mt, st, ht, xin, gst, wr, ur, wp, up,
                 ob, xa, mref, yo, gp, bm, zm, tm, wa,
                 a_sem, isend, irecv, wsend, wrecv, xsend, xrecv, fsend, frecv, gsend, grecv, osend, orecv):
    x, y, c = coords()
    partner = dev(x, y, 1 - c)
    greet()

    def init_piece(h):
        src = ens_ref.at[:, :, pl.ds(HALF * h, HALF)]
        dst = ht.at[:, pl.ds(pl.multiple_of(32 * y, 32), 32), :]
        is_self = jnp.logical_and(c == y, c == h)

        def local():
            return pltpu.make_async_copy(src, dst, irecv.at[y])

        def remote():
            return pltpu.make_async_remote_copy(src, dst, isend.at[h], irecv.at[y], device_id=dev(x, c, h), device_id_type=MESH)
        return is_self, local, remote

    weights = ((win_ref, wr), (wout_ref, ur))

    def weight_remote(n):
        src, dst = weights[n]
        return pltpu.make_async_remote_copy(src, dst.at[y], wsend.at[n], wrecv.at[n, 0], device_id=dev(x, 1 - y, c), device_id_type=MESH)

    def weight_local(n):
        src, dst = weights[n]
        return pltpu.make_async_copy(src, dst.at[y], wrecv.at[n, 1])

    for n in range(2):
        weight_remote(n).start()
        weight_local(n).start()
    for h in range(2):
        is_self, local, remote = init_piece(h)
        either(is_self, lambda: local().start(), lambda: remote().start())

    def a_copy(t, q):
        row = pl.multiple_of((4 * c + q) * BLK + LANE * t, LANE)
        return pltpu.make_async_copy(a_ref.at[pl.ds(row, LANE), :], a_vm.at[t, pl.ds(LANE * q, LANE), :], a_sem.at[t, q])

    for t in range(TILES):
        for q in range(4):
            a_copy(t, q).start()

    for n in range(2):
        weight_local(n).wait()
        weight_remote(n).wait()
    for layer in range(layers):
        for part in range(2):
            for p in range(2):
                lo = HID * p + 512 * part
                wv = (wr[part, layer].astype(F32) * 0.5).astype(BF16)
                wz = jnp.zeros_like(wv)
                wp[layer, :, lo:lo + 512] = jnp.concatenate([wv, wz] if p == 0 else [wz, wv], axis=0)
                uv = ur[part, layer].astype(F32)
                uz = jnp.zeros_like(uv)
                up[layer, lo:lo + 512, :] = jnp.concatenate([uv, uz] if p == 0 else [uz, uv], axis=0).T.astype(BF16)

    def share(buf, t):
        lane = pl.multiple_of(LANE * t, LANE)
        piece = hb.at[buf, pl.ds(4 * c, 4), pl.ds(lane, LANE), :]
        return pltpu.make_async_remote_copy(piece, piece, xsend.at[buf, t], xrecv.at[buf, t], device_id=partner, device_id_type=MESH)

    def await_share(buf, t):
        lane = pl.multiple_of(LANE * t, LANE)
        await_bytes(hb.at[buf, pl.ds(4 * (1 - c), 4), pl.ds(lane, LANE), :], xrecv.at[buf, t])

    mine = 4 * (2 * x + y)

    def f_ship(t, q):
        c2, y2 = q // 2, q % 2
        lane = pl.multiple_of(LANE * t, LANE)
        src = st.at[t, :, :, pl.ds(LANE * q, LANE)]
        dst = xin.at[pl.ds(mine, 4), :, pl.ds(lane, LANE)]
        is_self = jnp.logical_and(x == c, jnp.logical_and(c == c2, y == y2))
        rsem = frecv.at[t, 2 * x + y]

        def local():
            return pltpu.make_async_copy(src, dst, rsem)

        def remote():
            return pltpu.make_async_remote_copy(src, dst, fsend.at[t, q], rsem, device_id=dev(c, y2, c2), device_id_type=MESH)
        return is_self, local, remote

    block = 4 * x + 2 * c + y
    back = [(1, 1), (1, 0), (0, 1), (0, 0)]

    def g_ship(t, n):
        dx, dy = back[n]
        x2, y2 = (x + dx) % 2, (y + dy) % 2
        lane = pl.multiple_of((2 * c + y) * BLK + LANE * t, LANE)
        src = gst.at[t, pl.ds(4 * (2 * x2 + y2), 4), :, :]
        dst = ht.at[:, :, pl.ds(lane, LANE)]
        rsem = grecv.at[t, 2 * c + y]
        is_self = (x == c) if n == 3 else False

        def local():
            return pltpu.make_async_copy(src, dst, rsem)

        def remote():
            return pltpu.make_async_remote_copy(src, dst, gsend.at[t, n], rsem, device_id=dev(x2, y2, x), device_id_type=MESH)
        return is_self, local, remote

    def o_ship(t, n):
        r = 7 - n
        x2, y2, c2 = (x + r // 4) % 2, (y + (r // 2) % 2) % 2, (c + r % 2) % 2
        lane = pl.multiple_of(block * BLK + LANE * t, LANE)
        src = gst.at[t, pl.ds(4 * (2 * x2 + c2), 4), pl.ds(pl.multiple_of(32 * y2, 32), 32), :]
        dst = out_ref.at[:, :, pl.ds(lane, LANE)]
        rsem = orecv.at[t, block]

        def local():
            return pltpu.make_async_copy(src, dst, rsem)

        def remote():
            return pltpu.make_async_remote_copy(src, dst, osend.at[t, n], rsem, device_id=dev(x2, y2, c2), device_id_type=MESH)
        return r == 0, local, remote

    def start(ship):
        is_self, local, remote = ship
        either(is_self, lambda: local().start(), lambda: remote().start())

    def sent(ship):
        is_self, local, remote = ship
        either(is_self, lambda: None, lambda: remote().wait_send())

    def cycle_body(cycle, carry):
        first = lax.rem(cycle * layers, 2)

        @pl.when(cycle == 0)
        def _():
            for h in range(2):
                sent(init_piece(h))
            for s in range(2):
                await_bytes(ht.at[:, 32 * s:32 * s + 32, :], irecv.at[s])

        def load_body(t, carry2):
            @pl.when(cycle > 0)
            def _():
                for s in range(4):
                    await_bytes(ht.at[:, :, pl.ds(pl.multiple_of(BLK * s + LANE * t, LANE), LANE)], grecv.at[t, s])
            lane = pl.multiple_of(LANE * t, LANE)
            for q in range(4):
                part = ht[:, :, pl.ds(pl.multiple_of(BLK * q + lane, LANE), LANE)].reshape(4 * VARS, LANE).T
                hf[t, LANE * q:LANE * (q + 1), :] = part
                hb[first, 4 * c + q, pl.ds(lane, LANE), :] = part.astype(BF16)
            share(first, t).start()
            return carry2

        lax.fori_loop(0, TILES, load_body, 0)

        def layer_body(layer, carry2):
            cur = lax.rem(cycle * layers + layer, 2)
            nxt = 1 - cur
            for t in range(TILES):
                await_share(cur, t)
                share(cur, t).wait_send()

            def tile_body(t, carry3):
                @pl.when(jnp.logical_and(layer == 0, cycle == 0))
                def _():
                    for q in range(4):
                        a_copy(t, q).wait()
                state = hb[cur].reshape(COLS, 4 * VARS)
                for r in range(2):
                    mixed = jnp.dot(a_vm[t, 256 * r:256 * (r + 1), :], state, preferred_element_type=F32)
                    mt[256 * r:256 * (r + 1), :] = mixed.astype(BF16)
                sums = [None, None]
                for n in range(8):
                    for p in range(2):
                        lo = 256 * n
                        h = jnp.dot(mt[:, 128 * p:128 * (p + 1)], wp[layer, :, lo:lo + 256], preferred_element_type=F32)
                        z = h * (C1 + C2 * (h * h))
                        q_act = (h + h * jnp.tanh(z)).astype(BF16)
                        part = jnp.dot(q_act, up[layer, lo:lo + 256, :], preferred_element_type=F32)
                        sums[p] = part if sums[p] is None else sums[p] + part
                for p in range(2):
                    hf[t, :, 128 * p:128 * (p + 1)] = hf[t, :, 128 * p:128 * (p + 1)] + sums[p]

                @pl.when(layer < layers - 1)
                def _():
                    lane = pl.multiple_of(LANE * t, LANE)
                    for q in range(4):
                        hb[nxt, 4 * c + q, pl.ds(lane, LANE), :] = hf[t, LANE * q:LANE * (q + 1), :].astype(BF16)
                    share(nxt, t).start()

                @pl.when(layer == layers - 1)
                def _():
                    for q in range(4):
                        st[t, :, :, LANE * q:LANE * (q + 1)] = hf[t, LANE * q:LANE * (q + 1), :].T.reshape(4, VARS, LANE)
                    for q in range(4):
                        start(f_ship(t, q))
                return carry3

            return lax.fori_loop(0, TILES, tile_body, carry2)

        lax.fori_loop(0, layers, layer_body, 0)

        @pl.when(cycle > 0)
        def _():
            for t in range(TILES):
                for n in range(4):
                    sent(g_ship(t, n))

        def analysis_body(t, carry2):
            for s in range(4):
                await_bytes(xin.at[4 * s:4 * s + 4, :, pl.ds(pl.multiple_of(LANE * t, LANE), LANE)], frecv.at[t, s])

            def write(k, row, a, b):
                gst[t, k, row:row + 8, :] = a
                gst[t, k, row + 8:row + 16, :] = b
            analyse_tile(xin, t, idx_ref, obs_ref.at[cycle], prec_ref, rho_ref[0], ob, xa, mref, yo, gp, bm, zm, tm, wa, write)

            @pl.when(cycle < cycles - 1)
            def _():
                for n in range(4):
                    start(g_ship(t, n))

            @pl.when(cycle == cycles - 1)
            def _():
                for n in range(8):
                    start(o_ship(t, n))
            return carry2

        lax.fori_loop(0, TILES, analysis_body, 0)
        for t in range(TILES):
            for q in range(4):
                sent(f_ship(t, q))
        return carry

    lax.fori_loop(0, cycles, cycle_body, 0)
    for t in range(TILES):
        for n in range(8):
            sent(o_ship(t, n))
        for s in range(8):
            lo = BLK * s + LANE * t
            await_bytes(out_ref.at[:, :, lo:lo + LANE], orecv.at[t, s])


def run_cycles(ens_t, w_in, w_out_t, mix_op, obs_t, prec_t, obs_idx, rho):
    vm = pl.BlockSpec(memory_space=pltpu.VMEM)
    sm = pl.BlockSpec(memory_space=pltpu.SMEM)
    hbm = pl.BlockSpec(memory_space=pl.ANY)
    dma = pltpu.SemaphoreType.DMA
    layers, cycles = w_in.shape[0], obs_t.shape[0]
    return pl.pallas_call(
        functools.partial(cycle_kernel, layers, cycles),
        out_shape=jax.ShapeDtypeStruct((4, 32, COLS), F32),
        in_specs=[hbm, hbm, hbm, hbm, vm, vm, sm, sm],
        out_specs=hbm,
        scratch_shapes=[
            pltpu.VMEM((TILES, ROWS, COLS), BF16),
            pltpu.VMEM((2, 8, BLK, 4 * VARS), BF16),
            pltpu.VMEM((TILES, ROWS, 4 * VARS), F32),
            pltpu.VMEM((ROWS, 4 * VARS), BF16),
            pltpu.VMEM((TILES, 4, VARS, ROWS), F32),
            pltpu.VMEM((4, VARS, HALF), F32),
            pltpu.VMEM((K, VARS, BLK), F32),
            pltpu.VMEM((TILES, K, VARS, LANE), F32),
            pltpu.VMEM((2, layers, VARS, HID // 2), BF16),
            pltpu.VMEM((2, layers, VARS, HID // 2), BF16),
            pltpu.VMEM((layers, 2 * VARS, 2 * HID), BF16),
            pltpu.VMEM((layers, 2 * HID, 2 * VARS), BF16),
            pltpu.VMEM((64, LANE), F32),
            pltpu.VMEM((K * VARS, LANE), F32),
            pltpu.VMEM((VARS, LANE), F32),
            pltpu.VMEM((512, LANE), F32),
            pltpu.VMEM((512, LANE), F32),
            pltpu.VMEM((2, 256, LANE), F32),
            pltpu.VMEM((2, 256, LANE), F32),
            pltpu.VMEM((256, LANE), F32),
            pltpu.VMEM((256, LANE), F32),
            dma((TILES, 4)),
            dma((2,)),
            dma((2,)),
            dma((2,)),
            dma((2, 2)),
            dma((2, TILES)),
            dma((2, TILES)),
            dma((TILES, 4)),
            dma((TILES, 4)),
            dma((TILES, 4)),
            dma((TILES, 4)),
            dma((TILES, 8)),
            dma((TILES, 8)),
        ],
        compiler_params=pltpu.CompilerParams(collective_id=1, has_side_effects=True, vmem_limit_bytes=VMEM_LIMIT),
        name="cycle_all",
    )(ens_t, w_in, w_out_t, mix_op, obs_t, prec_t, obs_idx, rho)


def solution(mesh):
    def local_step(ens_local, mix_op, w_in, w_out, obs_val, obs_prec, obs_idx, inflation):
        out = run_cycles(
            jnp.transpose(ens_local, (0, 2, 1)), w_in, jnp.transpose(w_out, (0, 2, 1)), mix_op,
            jnp.transpose(obs_val, (0, 2, 1)), jnp.transpose(obs_prec, (1, 0)), obs_idx, inflation)
        return jnp.transpose(out, (0, 2, 1))

    member_spec = P(("case", "ens"), None, "model")
    col_axes = ("case", "ens", "model")
    in_specs = (member_spec, P(None, None), P(None, None, "model"), P(None, "model", None), P(None, col_axes, None), P(col_axes, None), P(None), P(None))
    return jax.shard_map(local_step, mesh=mesh, in_specs=in_specs, out_specs=member_spec, check_vma=False)
```

time: 378 us -> 270 us (0.71)
  Pallas kernels: 355 us -> 265 us
  local copies, waits for them, and re-layouts: 18.5 us -> 3.48 us
    pallas_call x5 -> x1, Pallas kernels: 355 us -> 265 us  [run_cycles(): pl.pallas_call(functools.partial(cycle_kernel, layers, cycles), out_shape...]
    unnamed x27 -> x1, local copies, waits for them, and re-layouts: 16.4 us -> 3.48 us
where the time goes in v3:
time: 270 us
  Pallas kernels  265 us (98%)
  local copies, waits for them, and re-layouts  3.48 us (1%)
    pallas_call x1, Pallas kernels, run_cycles(): pl.pallas_call(functools.partial(cycle_kernel, layers, cycles), out_shape...  265 us

profile of v3, /device:TPU:0, one launch (start us, length us, event | category | flops | bytes accessed | tf_op | source)
XLA Modules:
  0.0 269.5 jit_solution(9396305685377354043)
XLA Ops:
  0.7 265.4 %cycle_all.1 = f32[4,32,5120]{2,1,0:T(8,128)} custom-call(f32[4,32,5120]{2,1,0:T(8,128)} %bitcast.6, bf16[3,64,512]{2,1,0:T(8,128)(2,1)} %win_ref.1, bf16[3,64,512]{2,1,0:T(8,128)(2,1)} %bitcast.7, bf16[5120,5120]{1,0:T(8,128)(2,1)} %a_ref.1, f32[2,32,640]{2,1,0:T(8,128)} %bitcast.8, f32[32,640]{1,0:T(8,128)} %bitcast.9, s32[32]{0:T(128)} %idx_ref.1, ...), custom_call_target="tpu_custom_call" | custom-call | tf_op jit(solution)/shard_map/cycle_all/pallas_call | solution.py:474
  266.1 3.5 %copy.11 = f32[4,5120,32]{1,2,0:T(8,128)} copy(f32[4,5120,32]{1,2,0:T(8,128)} %bitcast.5) | data formatting | bytes 5242880

commit v4 on v3

--- a/solution.py
+++ b/solution.py
@@ -80,7 +80,7 @@
     sub = lax.broadcasted_iota(jnp.int32, (8, LANE), 0)
     for v in range(8):
         rows = slice(8 * v, 8 * v + 8)
-        vals = [xin[k, rows, lanes] for k in range(K)]
+        vals = [xin[t, k, rows, :] for k in range(K)]
         total = vals[0]
         for k in range(1, K):
             total = total + vals[k]
@@ -233,34 +233,37 @@
     partner = dev(x, y, 1 - c)
     greet()
 
-    def init_piece(h):
-        src = ens_ref.at[:, :, pl.ds(HALF * h, HALF)]
-        dst = ht.at[:, pl.ds(pl.multiple_of(32 * y, 32), 32), :]
+    def init_piece(h, t, q):
+        src = ens_ref.at[:, :, pl.ds(HALF * h + BLK * q + LANE * t, LANE)]
+        dst = ht.at[t, q, :, pl.ds(pl.multiple_of(32 * y, 32), 32), :]
         is_self = jnp.logical_and(c == y, c == h)
+        rsem = irecv.at[t, q, y]
 
         def local():
-            return pltpu.make_async_copy(src, dst, irecv.at[y])
+            return pltpu.make_async_copy(src, dst, rsem)
 
         def remote():
-            return pltpu.make_async_remote_copy(src, dst, isend.at[h], irecv.at[y], device_id=dev(x, c, h), device_id_type=MESH)
+            return pltpu.make_async_remote_copy(src, dst, isend.at[h, t, q], rsem, device_id=dev(x, c, h), device_id_type=MESH)
         return is_self, local, remote
 
     weights = ((win_ref, wr), (wout_ref, ur))
-
-    def weight_remote(n):
-        src, dst = weights[n]
-        return pltpu.make_async_remote_copy(src, dst.at[y], wsend.at[n], wrecv.at[n, 0], device_id=dev(x, 1 - y, c), device_id_type=MESH)
 
     def weight_local(n):
         src, dst = weights[n]
         return pltpu.make_async_copy(src, dst.at[y], wrecv.at[n, 1])
 
+    @pl.when(c == y)
+    def _():
+        for n, (src, dst) in enumerate(weights):
+            pltpu.make_async_remote_copy(src, dst.at[y], wsend.at[n], wrecv.at[n, 0], device_id=dev(x, 1 - y, c), device_id_type=MESH).start()
+
     for n in range(2):
-        weight_remote(n).start()
         weight_local(n).start()
-    for h in range(2):
-        is_self, local, remote = init_piece(h)
-        either(is_self, lambda: local().start(), lambda: remote().start())
+    for t in range(TILES):
+        for q in range(4):
+            for h in range(2):
+                is_self, local, remote = init_piece(h, t, q)
+                either(is_self, lambda: local().start(), lambda: remote().start())
 
     def a_copy(t, q):
         row = pl.multiple_of((4 * c + q) * BLK + LANE * t, LANE)
@@ -272,7 +275,15 @@
 
     for n in range(2):
         weight_local(n).wait()
-        weight_remote(n).wait()
+    for n, (src, dst) in enumerate(weights):
+        piece = dst.at[1 - y]
+        await_bytes(piece, wrecv.at[n, 0])
+
+        @pl.when(c != y)
+        def _():
+            pltpu.make_async_remote_copy(piece, piece, wsend.at[n], wrecv.at[n, 0], device_id=partner, device_id_type=MESH).start()
+    for n, (src, dst) in enumerate(weights):
+        await_bytes(dst.at[1 - y], wsend.at[n])
     for layer in range(layers):
         for part in range(2):
             for p in range(2):
@@ -297,9 +308,8 @@
 
     def f_ship(t, q):
         c2, y2 = q // 2, q % 2
-        lane = pl.multiple_of(LANE * t, LANE)
-        src = st.at[t, :, :, pl.ds(LANE * q, LANE)]
-        dst = xin.at[pl.ds(mine, 4), :, pl.ds(lane, LANE)]
+        src = st.at[t, q]
+        dst = xin.at[t, pl.ds(mine, 4)]
         is_self = jnp.logical_and(x == c, jnp.logical_and(c == c2, y == y2))
         rsem = frecv.at[t, 2 * x + y]
 
@@ -316,9 +326,8 @@
     def g_ship(t, n):
         dx, dy = back[n]
         x2, y2 = (x + dx) % 2, (y + dy) % 2
-        lane = pl.multiple_of((2 * c + y) * BLK + LANE * t, LANE)
         src = gst.at[t, pl.ds(4 * (2 * x2 + y2), 4), :, :]
-        dst = ht.at[:, :, pl.ds(lane, LANE)]
+        dst = ht.at[t, 2 * c + y]
         rsem = grecv.at[t, 2 * c + y]
         is_self = (x == c) if n == 3 else False
 
@@ -355,21 +364,20 @@
     def cycle_body(cycle, carry):
         first = lax.rem(cycle * layers, 2)
 
-        @pl.when(cycle == 0)
-        def _():
-            for h in range(2):
-                sent(init_piece(h))
-            for s in range(2):
-                await_bytes(ht.at[:, 32 * s:32 * s + 32, :], irecv.at[s])
-
         def load_body(t, carry2):
+            @pl.when(cycle == 0)
+            def _():
+                for q in range(4):
+                    for s in range(2):
+                        await_bytes(ht.at[t, q, :, 32 * s:32 * s + 32, :], irecv.at[t, q, s])
+
             @pl.when(cycle > 0)
             def _():
                 for s in range(4):
-                    await_bytes(ht.at[:, :, pl.ds(pl.multiple_of(BLK * s + LANE * t, LANE), LANE)], grecv.at[t, s])
+                    await_bytes(ht.at[t, s], grecv.at[t, s])
             lane = pl.multiple_of(LANE * t, LANE)
             for q in range(4):
-                part = ht[:, :, pl.ds(pl.multiple_of(BLK * q + lane, LANE), LANE)].reshape(4 * VARS, LANE).T
+                part = ht[t, q].reshape(4 * VARS, LANE).T
                 hf[t, LANE * q:LANE * (q + 1), :] = part
                 hb[first, 4 * c + q, pl.ds(lane, LANE), :] = part.astype(BF16)
             share(first, t).start()
@@ -377,22 +385,52 @@
 
         lax.fori_loop(0, TILES, load_body, 0)
 
+        @pl.when(cycle == 0)
+        def _():
+            for t in range(TILES):
+                for q in range(4):
+                    for h in range(2):
+                        sent(init_piece(h, t, q))
+
         def layer_body(layer, carry2):
             cur = lax.rem(cycle * layers + layer, 2)
             nxt = 1 - cur
-            for t in range(TILES):
+            late = TILES - 1
+            for t in range(late):
                 await_share(cur, t)
-                share(cur, t).wait_send()
-
-            def tile_body(t, carry3):
+
+            def await_rows(t):
                 @pl.when(jnp.logical_and(layer == 0, cycle == 0))
                 def _():
                     for q in range(4):
                         a_copy(t, q).wait()
+
+            def first_mix():
+                def lates(r, core):
+                    out = None
+                    for j in range(4):
+                        lo = pl.multiple_of((4 * core + j) * BLK + LANE * late, LANE)
+                        part = jnp.dot(a_vm[0, 256 * r:256 * (r + 1), pl.ds(lo, LANE)], hb[cur, 4 * core + j, LANE * late:, :], preferred_element_type=F32)
+                        out = part if out is None else out + part
+                    return out
+                early = []
+                for r in range(2):
+                    acc = None
+                    for b in range(8):
+                        part = jnp.dot(a_vm[0, 256 * r:256 * (r + 1), BLK * b:BLK * b + LANE * late], hb[cur, b, :LANE * late, :], preferred_element_type=F32)
+                        acc = part if acc is None else acc + part
+                    early.append(acc + lates(r, c))
+                await_share(cur, late)
+                for r in range(2):
+                    mt[256 * r:256 * (r + 1), :] = (early[r] + lates(r, 1 - c)).astype(BF16)
+
+            def full_mix(t):
                 state = hb[cur].reshape(COLS, 4 * VARS)
                 for r in range(2):
                     mixed = jnp.dot(a_vm[t, 256 * r:256 * (r + 1), :], state, preferred_element_type=F32)
                     mt[256 * r:256 * (r + 1), :] = mixed.astype(BF16)
+
+            def finish(t):
                 sums = [None, None]
                 for n in range(8):
                     for p in range(2):
@@ -415,12 +453,22 @@
                 @pl.when(layer == layers - 1)
                 def _():
                     for q in range(4):
-                        st[t, :, :, LANE * q:LANE * (q + 1)] = hf[t, LANE * q:LANE * (q + 1), :].T.reshape(4, VARS, LANE)
+                        st[t, q] = hf[t, LANE * q:LANE * (q + 1), :].T.reshape(4, VARS, LANE)
                     for q in range(4):
                         start(f_ship(t, q))
+
+            def tile_body(t, carry3):
+                await_rows(t)
+                full_mix(t)
+                finish(t)
                 return carry3
 
-            return lax.fori_loop(0, TILES, tile_body, carry2)
+            await_rows(0)
+            first_mix()
+            finish(0)
+            for t in range(TILES):
+                share(cur, t).wait_send()
+            return lax.fori_loop(1, TILES, tile_body, carry2)
 
         lax.fori_loop(0, layers, layer_body, 0)
 
@@ -432,7 +480,7 @@
 
         def analysis_body(t, carry2):
             for s in range(4):
-                await_bytes(xin.at[4 * s:4 * s + 4, :, pl.ds(pl.multiple_of(LANE * t, LANE), LANE)], frecv.at[t, s])
+                await_bytes(xin.at[t, 4 * s:4 * s + 4], frecv.at[t, s])
 
             def write(k, row, a, b):
                 gst[t, k, row:row + 8, :] = a
@@ -481,9 +529,9 @@
             pltpu.VMEM((2, 8, BLK, 4 * VARS), BF16),
             pltpu.VMEM((TILES, ROWS, 4 * VARS), F32),
             pltpu.VMEM((ROWS, 4 * VARS), BF16),
-            pltpu.VMEM((TILES, 4, VARS, ROWS), F32),
-            pltpu.VMEM((4, VARS, HALF), F32),
-            pltpu.VMEM((K, VARS, BLK), F32),
+            pltpu.VMEM((TILES, 4, 4, VARS, LANE), F32),
+            pltpu.VMEM((TILES, 4, 4, VARS, LANE), F32),
+            pltpu.VMEM((TILES, K, VARS, LANE), F32),
             pltpu.VMEM((TILES, K, VARS, LANE), F32),
             pltpu.VMEM((2, layers, VARS, HID // 2), BF16),
             pltpu.VMEM((2, layers, VARS, HID // 2), BF16),
@@ -499,8 +547,8 @@
             pltpu.VMEM((256, LANE), F32),
             pltpu.VMEM((256, LANE), F32),
             dma((TILES, 4)),
-            dma((2,)),
-            dma((2,)),
+            dma((2, TILES, 4)),
+            dma((TILES, 4, 2)),
             dma((2,)),
             dma((2, 2)),
             dma((2, TILES)),

time: 270 us -> 259 us (0.959)
  Pallas kernels: 265 us -> 255 us
    pallas_call x1, Pallas kernels: 265 us -> 255 us  [run_cycles(): pl.pallas_call(functools.partial(cycle_kernel, layers, cycles), out_shape...]
where the time goes in v4:
time: 259 us
  Pallas kernels  255 us (98%)
  local copies, waits for them, and re-layouts  3.48 us (1%)
    pallas_call x1, Pallas kernels, run_cycles(): pl.pallas_call(functools.partial(cycle_kernel, layers, cycles), out_shape...  255 us

profile of v4, /device:TPU:0, one launch (start us, length us, event | category | flops | bytes accessed | tf_op | source)
XLA Modules:
  0.0 258.9 jit_solution(17818674981300080256)
XLA Ops:
  0.7 254.7 %cycle_all.1 = f32[4,32,5120]{2,1,0:T(8,128)} custom-call(f32[4,32,5120]{2,1,0:T(8,128)} %bitcast.6, bf16[3,64,512]{2,1,0:T(8,128)(2,1)} %win_ref.1, bf16[3,64,512]{2,1,0:T(8,128)(2,1)} %bitcast.7, bf16[5120,5120]{1,0:T(8,128)(2,1)} %a_ref.1, f32[2,32,640]{2,1,0:T(8,128)} %bitcast.8, f32[32,640]{1,0:T(8,128)} %bitcast.9, s32[32]{0:T(128)} %idx_ref.1, ...), custom_call_target="tpu_custom_call" | custom-call | tf_op jit(solution)/shard_map/cycle_all/pallas_call | solution.py:522
  255.4 3.5 %copy.11 = f32[4,5120,32]{1,2,0:T(8,128)} copy(f32[4,5120,32]{1,2,0:T(8,128)} %bitcast.5) | data formatting | bytes 5242880

commit v5 on v4

--- a/solution.py
+++ b/solution.py
@@ -18,6 +18,7 @@
 TILES = 5
 ROWS = 512
 HALF = 2560
+CHUNK = 1024
 NS_STEPS = 12
 VMEM_LIMIT = 64 * 1024 * 1024 - 64 * 1024
 F32 = jnp.float32
@@ -226,7 +227,7 @@
 
 
 def cycle_kernel(layers, cycles, ens_ref, win_ref, wout_ref, a_ref, obs_ref, prec_ref, idx_ref, rho_ref, out_ref,
-                 a_vm, hb, hf, mt, st, ht, xin, gst, wr, ur, wp, up,
+                 a_vm, hb, hf, mt, macc, st, ht, xin, gst, wr, ur, wp, up,
                  ob, xa, mref, yo, gp, bm, zm, tm, wa,
                  a_sem, isend, irecv, wsend, wrecv, xsend, xrecv, fsend, frecv, gsend, grecv, osend, orecv):
     x, y, c = coords()
@@ -266,12 +267,16 @@
                 either(is_self, lambda: local().start(), lambda: remote().start())
 
     def a_copy(t, q):
-        row = pl.multiple_of((4 * c + q) * BLK + LANE * t, LANE)
-        return pltpu.make_async_copy(a_ref.at[pl.ds(row, LANE), :], a_vm.at[t, pl.ds(LANE * q, LANE), :], a_sem.at[t, q])
+        src = a_ref.at[pl.ds(pl.multiple_of(HALF * c, HALF), HALF), pl.ds(pl.multiple_of(BLK * q + LANE * t, LANE), LANE)]
+        return pltpu.make_async_copy(src, a_vm.at[:, pl.ds(pl.multiple_of(CHUNK * t + LANE * q, LANE), LANE)], a_sem.at[t, q])
 
     for t in range(TILES):
-        for q in range(4):
+        for q in range(8):
             a_copy(t, q).start()
+
+    def a_rows(t, r, lo, size):
+        cols = pl.ds(lo, size)
+        return jnp.concatenate([a_vm[pl.ds(pl.multiple_of(BLK * q + LANE * t, LANE), LANE), cols] for q in (2 * r, 2 * r + 1)], axis=0)
 
     for n in range(2):
         weight_local(n).wait()
@@ -296,13 +301,11 @@
                 up[layer, lo:lo + 512, :] = jnp.concatenate([uv, uz] if p == 0 else [uz, uv], axis=0).T.astype(BF16)
 
     def share(buf, t):
-        lane = pl.multiple_of(LANE * t, LANE)
-        piece = hb.at[buf, pl.ds(4 * c, 4), pl.ds(lane, LANE), :]
+        piece = hb.at[buf, t, pl.ds(4 * c, 4)]
         return pltpu.make_async_remote_copy(piece, piece, xsend.at[buf, t], xrecv.at[buf, t], device_id=partner, device_id_type=MESH)
 
     def await_share(buf, t):
-        lane = pl.multiple_of(LANE * t, LANE)
-        await_bytes(hb.at[buf, pl.ds(4 * (1 - c), 4), pl.ds(lane, LANE), :], xrecv.at[buf, t])
+        await_bytes(hb.at[buf, t, pl.ds(4 * (1 - c), 4)], xrecv.at[buf, t])
 
     mine = 4 * (2 * x + y)
 
@@ -375,14 +378,26 @@
             def _():
                 for s in range(4):
                     await_bytes(ht.at[t, s], grecv.at[t, s])
-            lane = pl.multiple_of(LANE * t, LANE)
             for q in range(4):
                 part = ht[t, q].reshape(4 * VARS, LANE).T
                 hf[t, LANE * q:LANE * (q + 1), :] = part
-                hb[first, 4 * c + q, pl.ds(lane, LANE), :] = part.astype(BF16)
+                hb[first, t, 4 * c + q] = part.astype(BF16)
             share(first, t).start()
+
+            @pl.when(cycle == 0)
+            def _():
+                for q in range(8):
+                    a_copy(t, q).wait()
+            await_share(first, t)
+            lo = pl.multiple_of(CHUNK * t, CHUNK)
+            state = hb[first, t].reshape(CHUNK, 4 * VARS)
+            for tt in range(TILES):
+                for r in range(2):
+                    add = jnp.dot(a_rows(tt, r, lo, CHUNK), state, preferred_element_type=F32)
+                    macc[tt, 256 * r:256 * (r + 1), :] = macc[tt, 256 * r:256 * (r + 1), :] + add
             return carry2
 
+        macc[...] = jnp.zeros_like(macc)
         lax.fori_loop(0, TILES, load_body, 0)
 
         @pl.when(cycle == 0)
@@ -392,33 +407,45 @@
                     for h in range(2):
                         sent(init_piece(h, t, q))
 
+        def finish(layer, t):
+            nxt = lax.rem(cycle * layers + layer + 1, 2)
+            sums = [None, None]
+            for n in range(8):
+                for p in range(2):
+                    lo = 256 * n
+                    h = jnp.dot(mt[:, 128 * p:128 * (p + 1)], wp[layer, :, lo:lo + 256], preferred_element_type=F32)
+                    z = h * (C1 + C2 * (h * h))
+                    q_act = (h + h * jnp.tanh(z)).astype(BF16)
+                    part = jnp.dot(q_act, up[layer, lo:lo + 256, :], preferred_element_type=F32)
+                    sums[p] = part if sums[p] is None else sums[p] + part
+            for p in range(2):
+                hf[t, :, 128 * p:128 * (p + 1)] = hf[t, :, 128 * p:128 * (p + 1)] + sums[p]
+
+            @pl.when(layer < layers - 1)
+            def _():
+                for q in range(4):
+                    hb[nxt, t, 4 * c + q] = hf[t, LANE * q:LANE * (q + 1), :].astype(BF16)
+                share(nxt, t).start()
+
+            @pl.when(layer == layers - 1)
+            def _():
+                for q in range(4):
+                    st[t, q] = hf[t, LANE * q:LANE * (q + 1), :].T.reshape(4, VARS, LANE)
+                for q in range(4):
+                    start(f_ship(t, q))
+
         def layer_body(layer, carry2):
             cur = lax.rem(cycle * layers + layer, 2)
-            nxt = 1 - cur
             late = TILES - 1
-            for t in range(late):
-                await_share(cur, t)
-
-            def await_rows(t):
-                @pl.when(jnp.logical_and(layer == 0, cycle == 0))
-                def _():
-                    for q in range(4):
-                        a_copy(t, q).wait()
+            early_size = CHUNK * late
 
             def first_mix():
                 def lates(r, core):
-                    out = None
-                    for j in range(4):
-                        lo = pl.multiple_of((4 * core + j) * BLK + LANE * late, LANE)
-                        part = jnp.dot(a_vm[0, 256 * r:256 * (r + 1), pl.ds(lo, LANE)], hb[cur, 4 * core + j, LANE * late:, :], preferred_element_type=F32)
-                        out = part if out is None else out + part
-                    return out
+                    lo = pl.multiple_of(early_size + 512 * core, 512)
+                    return jnp.dot(a_rows(0, r, lo, 512), hb[cur, late, pl.ds(4 * core, 4)].reshape(512, 4 * VARS), preferred_element_type=F32)
                 early = []
                 for r in range(2):
-                    acc = None
-                    for b in range(8):
-                        part = jnp.dot(a_vm[0, 256 * r:256 * (r + 1), BLK * b:BLK * b + LANE * late], hb[cur, b, :LANE * late, :], preferred_element_type=F32)
-                        acc = part if acc is None else acc + part
+                    acc = jnp.dot(a_rows(0, r, 0, early_size), hb[cur, :late].reshape(early_size, 4 * VARS), preferred_element_type=F32)
                     early.append(acc + lates(r, c))
                 await_share(cur, late)
                 for r in range(2):
@@ -427,50 +454,31 @@
             def full_mix(t):
                 state = hb[cur].reshape(COLS, 4 * VARS)
                 for r in range(2):
-                    mixed = jnp.dot(a_vm[t, 256 * r:256 * (r + 1), :], state, preferred_element_type=F32)
+                    mixed = jnp.dot(a_rows(t, r, 0, COLS), state, preferred_element_type=F32)
                     mt[256 * r:256 * (r + 1), :] = mixed.astype(BF16)
 
-            def finish(t):
-                sums = [None, None]
-                for n in range(8):
-                    for p in range(2):
-                        lo = 256 * n
-                        h = jnp.dot(mt[:, 128 * p:128 * (p + 1)], wp[layer, :, lo:lo + 256], preferred_element_type=F32)
-                        z = h * (C1 + C2 * (h * h))
-                        q_act = (h + h * jnp.tanh(z)).astype(BF16)
-                        part = jnp.dot(q_act, up[layer, lo:lo + 256, :], preferred_element_type=F32)
-                        sums[p] = part if sums[p] is None else sums[p] + part
-                for p in range(2):
-                    hf[t, :, 128 * p:128 * (p + 1)] = hf[t, :, 128 * p:128 * (p + 1)] + sums[p]
-
-                @pl.when(layer < layers - 1)
-                def _():
-                    lane = pl.multiple_of(LANE * t, LANE)
-                    for q in range(4):
-                        hb[nxt, 4 * c + q, pl.ds(lane, LANE), :] = hf[t, LANE * q:LANE * (q + 1), :].astype(BF16)
-                    share(nxt, t).start()
-
-                @pl.when(layer == layers - 1)
-                def _():
-                    for q in range(4):
-                        st[t, q] = hf[t, LANE * q:LANE * (q + 1), :].T.reshape(4, VARS, LANE)
-                    for q in range(4):
-                        start(f_ship(t, q))
-
             def tile_body(t, carry3):
-                await_rows(t)
                 full_mix(t)
-                finish(t)
+                finish(layer, t)
                 return carry3
 
-            await_rows(0)
+            for t in range(late):
+                await_share(cur, t)
             first_mix()
-            finish(0)
+            finish(layer, 0)
             for t in range(TILES):
                 share(cur, t).wait_send()
             return lax.fori_loop(1, TILES, tile_body, carry2)
 
-        lax.fori_loop(0, layers, layer_body, 0)
+        def first_layer(t, carry2):
+            mt[...] = macc[t].astype(BF16)
+            finish(cycle * 0, t)
+            return carry2
+
+        lax.fori_loop(0, TILES, first_layer, 0)
+        for t in range(TILES):
+            share(first, t).wait_send()
+        lax.fori_loop(1, layers, layer_body, 0)
 
         @pl.when(cycle > 0)
         def _():
@@ -525,10 +533,11 @@
         in_specs=[hbm, hbm, hbm, hbm, vm, vm, sm, sm],
         out_specs=hbm,
         scratch_shapes=[
-            pltpu.VMEM((TILES, ROWS, COLS), BF16),
-            pltpu.VMEM((2, 8, BLK, 4 * VARS), BF16),
+            pltpu.VMEM((HALF, COLS), BF16),
+            pltpu.VMEM((2, TILES, 8, LANE, 4 * VARS), BF16),
             pltpu.VMEM((TILES, ROWS, 4 * VARS), F32),
             pltpu.VMEM((ROWS, 4 * VARS), BF16),
+            pltpu.VMEM((TILES, ROWS, 4 * VARS), F32),
             pltpu.VMEM((TILES, 4, 4, VARS, LANE), F32),
             pltpu.VMEM((TILES, 4, 4, VARS, LANE), F32),
             pltpu.VMEM((TILES, K, VARS, LANE), F32),
@@ -546,7 +555,7 @@
             pltpu.VMEM((2, 256, LANE), F32),
             pltpu.VMEM((256, LANE), F32),
             pltpu.VMEM((256, LANE), F32),
-            dma((TILES, 4)),
+            dma((TILES, 8)),
             dma((2, TILES, 4)),
             dma((TILES, 4, 2)),
             dma((2,)),

time: 259 us -> 248 us (0.958)
  Pallas kernels: 255 us -> 244 us
    pallas_call x1, Pallas kernels: 255 us -> 244 us  [run_cycles(): pl.pallas_call(functools.partial(cycle_kernel, layers, cycles), out_shape...]
where the time goes in v5:
time: 248 us
  Pallas kernels  244 us (98%)
  local copies, waits for them, and re-layouts  3.48 us (1%)
    pallas_call x1, Pallas kernels, run_cycles(): pl.pallas_call(functools.partial(cycle_kernel, layers, cycles), out_shape...  244 us

profile of v5, /device:TPU:0, one launch (start us, length us, event | category | flops | bytes accessed | tf_op | source)
XLA Modules:
  0.0 248.2 jit_solution(14516359958697033137)
XLA Ops:
  0.7 244.1 %cycle_all.1 = f32[4,32,5120]{2,1,0:T(8,128)} custom-call(f32[4,32,5120]{2,1,0:T(8,128)} %bitcast.6, bf16[3,64,512]{2,1,0:T(8,128)(2,1)} %win_ref.1, bf16[3,64,512]{2,1,0:T(8,128)(2,1)} %bitcast.7, bf16[5120,5120]{1,0:T(8,128)(2,1)} %a_ref.1, f32[2,32,640]{2,1,0:T(8,128)} %bitcast.8, f32[32,640]{1,0:T(8,128)} %bitcast.9, s32[32]{0:T(128)} %idx_ref.1, ...), custom_call_target="tpu_custom_call" | custom-call | tf_op jit(solution)/shard_map/cycle_all/pallas_call | solution.py:530
  244.8 3.5 %copy.11 = f32[4,5120,32]{1,2,0:T(8,128)} copy(f32[4,5120,32]{1,2,0:T(8,128)} %bitcast.5) | data formatting | bytes 5242880
